TPU v7x, 512 devices: a whole 4x4x16 slice. The times are simulated.
512 devices in a mesh: tm: 128 (over z, x, core), space: 4 (over y).
Axes of the slice: x: 4, y: 4, z: 16, core: 2. Of those that a mesh axis runs over, the one named last changes fastest.
Arguments:
- state: float32 [512, 16, 64, 128], P('tm', 'space'), may hold values from -6 to 6
- source: float32 [512, 16, 64, 128], P('tm', 'space'), may hold values from -6 to 6
- absorption: float32 [16, 64, 128], P('space'), may hold values from 0.05 to 0.5
Outputs:
- relaxed: float32 [512, 16, 64, 128], P('tm', 'space')
- coarse_residual: float32 [128, 16, 64, 128], P('tm', 'space')
- residual_norm: float32 [], replicated
All inputs are finite; a program needn't handle non-finite values.
Results may differ from a plain program's by a relative error of at most 0.0004.
Values sent between devices are 32-bit elements; how exact they have to be, the bound alone decides.
A program may use at most 64 MiB of HBM per device.

v0:
```python
import math

import jax
import jax.numpy as jnp
from jax import lax
from jax.sharding import Mesh
from jax.sharding import PartitionSpec as P

CF = 4
SWEEPS = 5
TM = ("tm_0", "tm_1", "tm_2")
TM_SPACE = ("tm_0", "tm_1", "tm_2", "space")


coupling = 4.0


def shifted(value, axis, by):
    count = lax.axis_size(axis)
    pairs = [(i, i + by) for i in range(count) if 0 <= i + by < count]
    return lax.ppermute(value, axis, pairs)


def laid_out(tiles, dim):
    shape = list(tiles.shape[1:])
    shape[dim] *= tiles.shape[0]
    return jnp.moveaxis(tiles, 0, dim).reshape(shape)


def sent_to_all(value, axis):
    count = lax.axis_size(axis)
    return lax.all_to_all(
        jnp.broadcast_to(value[None], (count, *value.shape)), axis, 0, 0, tiled=True
    )


def collect(value, axis, dim):
    return laid_out(sent_to_all(value, axis), dim)


def by_axis(value, axes):
    for axis in axes:
        value = lax.psum(value, axis)
    return value


def sweep_weights(count):
    spread = 6.0 * coupling / (1.0 + 6.0 * coupling)
    return [
        1.0 / (1.0 + spread * math.cos(math.pi * (2 * k + 1) / (2 * count))) for k in range(count)
    ]


def apply_inner(extended, diag):
    inner = extended[1:-1]
    sides = jnp.pad(inner, ((0, 0), (1, 1), (1, 1)))
    beside = extended[2:] + extended[:-2]
    beside = beside + sides[:, 2:, 1:-1] + sides[:, :-2, 1:-1]
    beside = beside + sides[:, 1:-1, 2:] + sides[:, 1:-1, :-2]
    return diag * inner - coupling * beside


def step_whole(rhs, diag_full):
    field = rhs / diag_full
    for weight in sweep_weights(SWEEPS):
        extended = jnp.pad(field, ((1, 1), (0, 0), (0, 0)))
        field = field + weight * (rhs - apply_inner(extended, diag_full)) / diag_full
    return field


def local(state, source, absorption):
    depth_cells = absorption.shape[0]
    offset = lax.axis_index("space") * depth_cells

    def previous(last):
        return shifted(last, TM, 1)

    stacked = jnp.concatenate([state[:1], source, absorption[None]], axis=0)
    gathered = collect(stacked, "space", 1)
    source_full = gathered[1 : CF + 1]
    diag_full = 1.0 + 6.0 * coupling + gathered[CF + 1]

    def own_layers(field):
        return lax.dynamic_slice_in_dim(field, offset, depth_cells, 0)

    def back_full(last):
        return collect(previous(own_layers(last)), "space", 0)

    points = [gathered[0]] + [None] * (CF - 1)

    def relax_full(points):
        for j in range(1, CF):
            points[j] = step_whole(points[j - 1], diag_full) + source_full[j]
        return points

    points = relax_full(points)
    points[0] = step_whole(back_full(points[-1]), diag_full) + source_full[0]
    points = relax_full(points)
    coarse_full = source_full[0] + step_whole(back_full(points[-1]), diag_full) - points[0]
    coarse_residual = own_layers(coarse_full)
    points = [own_layers(point) for point in points]
    residual_norm = by_axis(jnp.sum(coarse_residual * coarse_residual), TM_SPACE)
    relaxed = jnp.stack(points, axis=0)
    return (relaxed, coarse_residual[None], residual_norm)


def solution(mesh):
    finer = Mesh(
        mesh.devices.reshape(16, 4, 2, mesh.shape["space"]), ("tm_0", "tm_1", "tm_2", "space")
    )
    return jax.shard_map(
        local,
        mesh=finer,
        in_specs=(P(TM, "space", None, None), P(TM, "space", None, None), P("space", None, None)),
        out_specs=(P(TM, "space", None, None), P(TM, "space", None, None), P()),
        check_vma=False,
    )
```

profile of v0, /device:TPU:1, one launch (start us, length us, event | category | flops | bytes accessed | tf_op | source)
XLA Modules:
  0.0 162.3 jit_solution(5410816493156166296)
XLA Ops:
  0.6 0.9 slice.797
  1.5 1.2 pad_maximum_fusion
  2.7 2.1 %broadcast_in_dim.11 = f32[4,6,4,64,128]{4,3,2,1,0:T(8,128)} broadcast(f32[6,4,64,128]{3,2,1,0:T(8,128)S(1)} %pad_maximum_fusion), dimensions={1,2,3,4} | broadcast | bytes 3932160 | tf_op jit(solution)/shard_map/broadcast_in_dim | solution.py:33
  4.8 5.0 %all-to-all-start = ((f32[4,6,4,64,128]{4,3,2,1,0:T(8,128)}), f32[4,6,4,64,128]{4,3,2,1,0:T(8,128)S(1)}, u32[]{:S(2)}, u32[]{:S(2)}) async-start(f32[4,6,4,64,128]{4,3,2,1,0:T(8,128)} %broadcast_in_dim.11), calls=%async_computation | async-start | bytes 6291456 | tf_op jit(solution)/shard_map/all_to_all | solution.py:32
  9.8 32.2 %all-to-all-done = f32[4,6,4,64,128]{4,3,2,1,0:T(8,128)S(1)} async-done(((f32[4,6,4,64,128]{4,3,2,1,0:T(8,128)}), f32[4,6,4,64,128]{4,3,2,1,0:T(8,128)S(1)}, u32[]{:S(2)}, u32[]{:S(2)}) %all-to-all-start) | async-done | bytes 3145760 | tf_op jit(solution)/shard_map/all_to_all | solution.py:32
  42.4 0.4 fusion.10
  42.9 0.4 fusion.21
  43.3 0.4 fusion.31
  43.7 0.4 fusion.42
  44.2 0.5 bitcast_divide_fusion.7
  44.6 0.4 fusion.65
  45.1 0.4 fusion.76
  45.5 0.4 fusion.86
  46.0 0.4 fusion.97
  46.4 0.5 bitcast_divide_fusion.5
  46.8 0.4 fusion.120
  47.7 0.4 fusion.141
  48.2 0.5 bitcast_multiply_fusion
  49.0 9.4 %collective-permute-start = (f32[4,64,128]{2,1,0:T(8,128)S(1)}, f32[4,64,128]{2,1,0:T(8,128)S(1)}, u32[]{:S(2)}, u32[]{:S(2)}) collective-permute-start(f32[4,64,128]{2,1,0:T(8,128)S(1)} %fusion.430), channel_id=1, source_target_pairs={{0,4},{4,8},{8,12},{12,16},{16,20},{20,24},{24,28},{28,32},{32,36}... | collective-permute-start | bytes 393224 | tf_op jit(solution)/shard_map/ppermute | solution.py:21
  58.4 1.9 %collective-permute-done = f32[4,64,128]{2,1,0:T(8,128)S(1)} collective-permute-done((f32[4,64,128]{2,1,0:T(8,128)S(1)}, f32[4,64,128]{2,1,0:T(8,128)S(1)}, u32[]{:S(2)}, u32[]{:S(2)}) %collective-permute-start) | collective-permute-done | bytes 131104 | tf_op jit(solution)/shard_map/ppermute | solution.py:21
  60.4 9.9 %all_to_all.15 = f32[4,4,64,128]{3,2,1,0:T(8,128)S(1)} all-to-all(f32[4,4,64,128]{3,2,1,0:T(8,128)S(1)} %broadcast_in_dim.12), channel_id=1, replica_groups=mesh['tm_0'=16,'tm_1'=4,'tm_2'=2,'space'=4] {'space'}, dimensions={0} | all-to-all | bytes 1048576 | tf_op jit(solution)/shard_map/all_to_all | solution.py:32
  70.8 0.4 fusion.180
  71.3 0.4 fusion.190
  71.7 0.4 fusion.201
  72.2 0.5 bitcast_divide_fusion.3
  72.6 0.4 fusion.224
  73.5 0.4 fusion.245
  73.9 0.4 fusion.256
  74.4 0.4 bitcast_divide_fusion.6
  75.7 0.4 fusion.300
  76.5 0.4 bitcast_divide_fusion.4
  77.0 0.4 fusion.334
  77.4 0.4 fusion.345
  77.8 0.4 fusion.355
  78.3 0.5 bitcast_multiply_fusion.1
  79.2 5.9 %collective-permute-start.1 = (f32[4,64,128]{2,1,0:T(8,128)S(1)}, f32[4,64,128]{2,1,0:T(8,128)S(1)}, u32[]{:S(2)}, u32[]{:S(2)}) collective-permute-start(f32[4,64,128]{2,1,0:T(8,128)S(1)} %get-tuple-element.27), channel_id=1, source_target_pairs={{0,4},{4,8},{8,12},{12,16},{16,20},{20,24},{24,28},{28,32},{32,36}... | collective-permute-start | bytes 393224 | tf_op jit(solution)/shard_map/ppermute | solution.py:21
  85.1 1.9 %collective-permute-done.1 = f32[4,64,128]{2,1,0:T(8,128)S(1)} collective-permute-done((f32[4,64,128]{2,1,0:T(8,128)S(1)}, f32[4,64,128]{2,1,0:T(8,128)S(1)}, u32[]{:S(2)}, u32[]{:S(2)}) %collective-permute-start.1) | collective-permute-done | bytes 131104 | tf_op jit(solution)/shard_map/ppermute | solution.py:21
  87.1 9.3 %all_to_all.16 = f32[4,4,64,128]{3,2,1,0:T(8,128)S(1)} all-to-all(f32[4,4,64,128]{3,2,1,0:T(8,128)S(1)} %broadcast_in_dim.13), channel_id=1, replica_groups=mesh['tm_0'=16,'tm_1'=4,'tm_2'=2,'space'=4] {'space'}, dimensions={0} | all-to-all | bytes 1048576 | tf_op jit(solution)/shard_map/all_to_all | solution.py:32
  96.5 0.4 fusion.383
  97.0 0.4 fusion.394
  97.4 0.4 fusion.404
  97.9 0.4 fusion.415
  98.7 1.3 multiply_reduce_fusion
  100.0 29.9 %psum.28 = f32[]{:T(128)} all-reduce(f32[]{:T(128)} %get-tuple-element.3), channel_id=1, replica_groups=mesh['tm_0'=16,'tm_1'=4,'tm_2'=2,'space'=4] {'tm_0'}, use_global_device_ids=true, to_apply=%region_1.2 | all-reduce | flops 1 | bytes 8 | tf_op jit(solution)/shard_map/psum | solution.py:43
  129.9 11.9 %psum.29 = f32[]{:T(128)} all-reduce(f32[]{:T(128)} %psum.28), channel_id=1, replica_groups=mesh['tm_0'=16,'tm_1'=4,'tm_2'=2,'space'=4] {'tm_1'}, use_global_device_ids=true, to_apply=%region_2.3 | all-reduce | flops 1 | bytes 8 | tf_op jit(solution)/shard_map/psum | solution.py:43
  141.8 12.2 %psum.30 = f32[]{:T(128)} all-reduce(f32[]{:T(128)} %psum.29), channel_id=1, replica_groups=mesh['tm_0'=16,'tm_1'=4,'tm_2'=2,'space'=4] {'tm_2'}, use_global_device_ids=true, to_apply=%region_3.4 | all-reduce | flops 1 | bytes 8 | tf_op jit(solution)/shard_map/psum | solution.py:43
  153.9 7.5 %psum.31 = f32[]{:T(128)} all-reduce(f32[]{:T(128)} %psum.30), channel_id=1, replica_groups=mesh['tm_0'=16,'tm_1'=4,'tm_2'=2,'space'=4] {'space'}, use_global_device_ids=true, to_apply=%region_4.5 | all-reduce | flops 1 | bytes 8 | tf_op jit(solution)/shard_map/psum | solution.py:43
  161.5 0.8 pad_maximum_fusion.1
  (18 shorter events, 4.4 us)
Async XLA Ops:
  4.8 37.2 %all-to-all-start = ((f32[4,6,4,64,128]{4,3,2,1,0:T(8,128)}), f32[4,6,4,64,128]{4,3,2,1,0:T(8,128)S(1)}, u32[]{:S(2)}, u32[]{:S(2)}) async-start(f32[4,6,4,64,128]{4,3,2,1,0:T(8,128)} %broadcast_in_dim.11), calls=%async_computation | async-start | bytes 6291456 | tf_op jit(solution)/shard_map/all_to_all | solution.py:32
  49.0 11.3 %collective-permute-start = (f32[4,64,128]{2,1,0:T(8,128)S(1)}, f32[4,64,128]{2,1,0:T(8,128)S(1)}, u32[]{:S(2)}, u32[]{:S(2)}) collective-permute-start(f32[4,64,128]{2,1,0:T(8,128)S(1)} %fusion.430), channel_id=1, source_target_pairs={{0,4},{4,8},{8,12},{12,16},{16,20},{20,24},{24,28},{28,32},{32,36}... | collective-permute-start | bytes 393224 | tf_op jit(solution)/shard_map/ppermute | solution.py:21
  79.2 7.8 %collective-permute-start.1 = (f32[4,64,128]{2,1,0:T(8,128)S(1)}, f32[4,64,128]{2,1,0:T(8,128)S(1)}, u32[]{:S(2)}, u32[]{:S(2)}) collective-permute-start(f32[4,64,128]{2,1,0:T(8,128)S(1)} %get-tuple-element.27), channel_id=1, source_target_pairs={{0,4},{4,8},{8,12},{12,16},{16,20},{20,24},{24,28},{28,32},{32,36}... | collective-permute-start | bytes 393224 | tf_op jit(solution)/shard_map/ppermute | solution.py:21
where the time goes:
time: 164 us; the launch traced here: 162 us
  blocking collectives  80.7 us (49%)
  waiting for transfers between devices  36 us (22%)
  other arithmetic  21.2 us (13%)
  starting transfers between devices  20.3 us (12%)
  local copies, waits for them, and re-layouts  3.06 us (2%)
    psum x4, blocking collectives, by_axis(): value = lax.psum(value, axis)  61.5 us
    all_to_all x1, waiting for transfers between devices, sent_to_all(): lax.all_to_all(jnp.broadcast_to(value[None], (count, *value.shape)), axis...  32.2 us
    all_to_all x2, blocking collectives, sent_to_all(): lax.all_to_all(jnp.broadcast_to(value[None], (count, *value.shape)), axis...  19.3 us
    ppermute x2, starting transfers between devices, shifted(): return lax.ppermute(value, axis, pairs)  15.3 us
    add x30, other arithmetic, step_whole(): field + weight * (rhs - apply_inner(extended, diag_full)) / diag_full  12.9 us
    all_to_all x1, starting transfers between devices, sent_to_all(): lax.all_to_all(jnp.broadcast_to(value[None], (count, *value.shape)), axis...  5 us
    ppermute x2, waiting for transfers between devices, shifted(): return lax.ppermute(value, axis, pairs)  3.85 us
  transfers between devices with their start and end apart: 3, of which 3 were waited for; matrix products, arithmetic and copies ran while one was open for 0% of the time, Pallas kernels for 0%

commit v1 on v0

v1 whole, which is shorter than its diff:
```python
import math

import jax
import jax.numpy as jnp
import numpy as np
from jax import lax
from jax.experimental import pallas as pl
from jax.experimental.pallas import tpu as pltpu
from jax.sharding import PartitionSpec as P

MESH = pl.DeviceIdType.MESH
CF = 4
SWEEPS = 5
COUPLING = 4.0
NZ, NX, NY = 16, 64, 128
OWN = 4
SPACES = 4
PLANE = 8


def sweep_weights(count):
    spread = 6.0 * COUPLING / (1.0 + 6.0 * COUPLING)
    return [
        1.0 / (1.0 + spread * math.cos(math.pi * (2 * k + 1) / (2 * count))) for k in range(count)
    ]


def coefficients():
    poly = np.zeros(SWEEPS + 1)
    poly[0] = 1.0
    for w in sweep_weights(SWEEPS):
        shifted = np.concatenate([[0.0], poly[:-1]])
        poly = (1.0 - w) * poly + w * shifted
        poly[0] += w
    return [float(c) for c in poly]


COEF = coefficients()
C2 = 0.5 * (COEF[2] + COEF[3])
C4 = 0.5 * (COEF[4] + COEF[5])


def kernel(
    state, source, absorption, relaxed, residual, norm,
    a_full, u_full, s1_full, s2_full, s0_own, s3_own,
    rd, q1, q2, q3, d_buf, p_buf, w_buf, v_buf, e_full, x_buf,
    rs_left, rs_right, rv_own, rv_left, rv_right, stage, r_recv, r_stage,
    na, nb,
    local_sem, out_sem, ag_send, ag_recv, rs_send, rs_recv, v_send, v_recv,
    r_send, r_recv_sem, na_send, na_recv, nb_send, nb_recv,
):
    c = lax.axis_index("tm")
    d = lax.axis_index("space")
    tms = lax.axis_size("tm")
    levels = tms // PLANE
    after, before = lax.rem(c + 1, tms), lax.rem(c + tms - 1, tms)
    right, left = lax.rem(d + 1, SPACES), lax.rem(d + SPACES - 1, SPACES)
    opposite = lax.rem(d + 2, SPACES)
    plane, seat = c // PLANE, lax.rem(c, PLANE)
    base = d * OWN

    def at(t, s):
        return {"tm": t, "space": s}

    def seat_at(i):
        return plane * PLANE + lax.rem(seat + i, PLANE)

    def level_at(i):
        return lax.rem(plane + i, levels) * PLANE + seat

    mine = pl.ds(base, OWN)
    loads = []
    for i, (src, dst) in enumerate([
        (absorption, a_full.at[mine]),
        (state.at[0], u_full.at[mine]),
        (source.at[1], s1_full.at[mine]),
        (source.at[2], s2_full.at[mine]),
        (source.at[0], s0_own),
        (source.at[3], s3_own),
    ]):
        copy = pltpu.make_async_copy(src, dst, local_sem.at[i])
        copy.start()
        loads.append(copy)

    barrier = pltpu.get_barrier_semaphore()
    peers = [at(c, left), at(c, right)]
    peers += [at(t, s) for t in (after, before) for s in (d, left, right)]
    peers += [at(seat_at(i), d) for i in range(1, PLANE)]
    peers += [at(level_at(i), d) for i in range(1, levels)]
    for peer in peers:
        pl.semaphore_signal(barrier, inc=1, device_id=peer, device_id_type=MESH)

    rows = lax.broadcasted_iota(jnp.int32, (8, NY), 0)
    lanes = lax.broadcasted_iota(jnp.int32, (8, 8, NY), 2)

    def natural(ref, *index):
        return jnp.stack([ref[(*index, pl.ds(v, 8, stride=8), slice(None))] for v in range(8)])

    def put_natural(ref, value, *index):
        for v in range(8):
            ref[(*index, pl.ds(v, 8, stride=8), slice(None))] = value[v]

    class Gather:
        def __init__(self, full, slot):
            self.full, self.slot = full, slot

        def copy(self, layers, part, target):
            return pltpu.make_async_remote_copy(
                src_ref=self.full.at[layers], dst_ref=self.full.at[layers],
                send_sem=ag_send.at[self.slot, part], recv_sem=ag_recv.at[self.slot, part],
                device_id=target, device_id_type=MESH,
            )

        def start(self):
            self.to_right = self.copy(mine, 0, at(c, right))
            self.to_left = self.copy(mine, 1, at(c, left))
            self.to_right.start()
            self.to_left.start()

        def forward(self):
            self.copy(pl.ds(left * OWN, OWN), 0, at(c, right)).wait_recv()
            self.on_right = self.copy(pl.ds(left * OWN, 2), 2, at(c, right))
            self.on_right.start()
            self.copy(pl.ds(right * OWN, OWN), 1, at(c, left)).wait_recv()
            self.on_left = self.copy(pl.ds(right * OWN + 2, 2), 3, at(c, left))
            self.on_left.start()

        def finish(self):
            self.copy(pl.ds(opposite * OWN, 2), 2, at(c, right)).wait_recv()
            self.copy(pl.ds(opposite * OWN + 2, 2), 3, at(c, left)).wait_recv()

        def drain(self):
            for copy in (self.to_right, self.to_left, self.on_right, self.on_left):
                copy.wait_send()

    gather_a, gather_u = Gather(a_full, 0), Gather(u_full, 1)
    gather_s1, gather_s2 = Gather(s1_full, 2), Gather(s2_full, 3)
    gather_e = Gather(e_full, 4)

    def neighbours(ref, z):
        x = ref[z]
        up = jnp.where(rows == 0, 0.0, pltpu.roll(x[7], 1, 0))
        down = jnp.where(rows == 7, 0.0, pltpu.roll(x[0], 7, 0))
        total = jnp.concatenate([up[None], x[:7]]) + jnp.concatenate([x[1:], down[None]])
        total = total + jnp.where(lanes == 0, 0.0, pltpu.roll(x, 1, 2))
        total = total + jnp.where(lanes == NY - 1, 0.0, pltpu.roll(x, NY - 1, 2))
        if z > 0:
            total = total + ref[z - 1]
        if z < NZ - 1:
            total = total + ref[z + 1]
        return x, total

    def phi(emit):
        for z in range(NZ):
            p_buf[z] = q1[z] * neighbours(d_buf, z)[1]
        for z in range(NZ):
            w_buf[z] = d_buf[z] + q2[z] * neighbours(p_buf, z)[1]
        for z in range(NZ):
            p_buf[z] = q1[z] * neighbours(w_buf, z)[1]
        for z in range(NZ):
            w_buf[z] = d_buf[z] + q3[z] * neighbours(p_buf, z)[1]
        for z in range(NZ):
            x, total = neighbours(w_buf, z)
            emit(z, x + q1[z] * total)

    loads[0].wait()
    pl.semaphore_wait(barrier, len(peers))

    gather_a.start()
    for load in loads[1:]:
        load.wait()
    for z in range(NZ):
        d_buf[z] = jnp.zeros((8, 8, NY), jnp.float32)
    gather_a.forward()
    gather_u.start()
    gather_a.finish()
    for z in range(NZ):
        inverse = 1.0 / (1.0 + 6.0 * COUPLING + natural(a_full, z))
        rd[z] = inverse
        q1[z] = COUPLING * inverse
        q2[z] = (COUPLING * C4 / C2) * inverse
        q3[z] = (COUPLING * C2) * inverse

    for k in range(OWN):
        d_buf[base + k] = rd[base + k] * natural(u_full, base + k)

    def scaled(z, x):
        d_buf[z] = rd[z] * x

    for own in (
        lambda k: natural(s1_full, base + k),
        lambda k: natural(s2_full, base + k),
        lambda k: natural(s3_own, k),
    ):
        phi(scaled)
        for k in range(OWN):
            d_buf[base + k] = d_buf[base + k] + rd[base + k] * own(k)

    def respond(z, x):
        v_buf[z] = x

    phi(respond)
    gather_u.forward()

    def remote(src, dst, send, recv, target):
        return pltpu.make_async_remote_copy(
            src_ref=src, dst_ref=dst, send_sem=send, recv_sem=recv,
            device_id=target, device_id_type=MESH,
        )

    part_right = remote(v_buf.at[pl.ds(opposite * OWN, 2)], rs_left,
                        rs_send.at[0], rs_recv.at[0], at(c, right))
    part_left = remote(v_buf.at[pl.ds(opposite * OWN + 2, 2)], rs_right,
                       rs_send.at[1], rs_recv.at[1], at(c, left))
    part_right.start()
    part_left.start()
    v_own = remote(v_buf.at[mine], rv_own, v_send.at[0], v_recv.at[0], at(after, d))
    v_own.start()
    v_right_late = remote(v_buf.at[pl.ds(right * OWN + 2, 2)], rv_left.at[pl.ds(2, 2)],
                          v_send.at[1], v_recv.at[1], at(after, right))
    v_left_late = remote(v_buf.at[pl.ds(left * OWN, 2)], rv_right.at[pl.ds(0, 2)],
                         v_send.at[2], v_recv.at[2], at(after, left))
    v_right_late.start()
    v_left_late.start()
    part_right.wait_recv()
    for k in range(2):
        v_buf[right * OWN + k] = v_buf[right * OWN + k] + rs_left[k]
    v_right = remote(v_buf.at[pl.ds(right * OWN, 2)], rv_left.at[pl.ds(0, 2)],
                     v_send.at[3], v_recv.at[3], at(after, right))
    v_right.start()
    part_left.wait_recv()
    for k in range(2):
        v_buf[left * OWN + 2 + k] = v_buf[left * OWN + 2 + k] + rs_right[k]
    v_left = remote(v_buf.at[pl.ds(left * OWN + 2, 2)], rv_right.at[pl.ds(2, 2)],
                    v_send.at[4], v_recv.at[4], at(after, left))
    v_left.start()

    gather_u.finish()
    for z in range(NZ):
        d_buf[z] = rd[z] * natural(u_full, z)

    def first(z, x):
        x_buf[4, z] = x

    phi(first)

    for copy in (v_own, v_right_late, v_left_late, v_right, v_left):
        copy.wait_recv()
    has_before = jnp.where(c > 0, 1.0, 0.0).astype(jnp.float32)
    for k in range(OWN):
        q = has_before * (rv_own[k] + rv_left[k] + rv_right[k])
        point = q + natural(s0_own, k)
        put_natural(stage, point, 0, k)
        e_full[base + k] = point - natural(u_full, base + k)
    gather_e.start()
    outs = [pltpu.make_async_copy(stage.at[0], relaxed.at[0], out_sem.at[0])]
    outs[0].start()
    gather_e.forward()
    gather_s1.start()
    gather_e.finish()

    for z in range(NZ):
        d_buf[z] = rd[z] * e_full[z]

    def chain(j):
        def emit(z, x):
            x_buf[j, z] = x
            d_buf[z] = rd[z] * x
        return emit

    for j in range(CF - 1):
        phi(chain(j))

    squares = []

    def last(z, x):
        x_buf[3, z] = x
        squares.append(x * x)

    phi(last)
    total = squares[0]
    for square in squares[1:]:
        total = total + square
    has_after = jnp.where(c < tms - 1, 1.0, 0.0).astype(jnp.float32)
    na[0] = has_after * jnp.sum(jnp.sum(total, axis=0), axis=0, keepdims=True)
    na_copies = []
    for i in range(1, PLANE):
        copy = remote(na.at[0], na.at[i], na_send.at[i - 1], na_recv.at[i - 1], at(seat_at(i), d))
        copy.start()
        na_copies.append(copy)
    r_copy = remote(x_buf.at[3, mine], r_recv, r_send.at[0], r_recv_sem.at[0], at(after, d))
    r_copy.start()
    gather_s1.forward()
    gather_s2.start()
    for copy in na_copies:
        copy.wait_recv()
    row = na[0]
    for i in range(1, PLANE):
        row = row + na[i]
    nb[0] = row
    nb_copies = []
    for i in range(1, levels):
        copy = remote(nb.at[0], nb.at[i], nb_send.at[i - 1], nb_recv.at[i - 1], at(level_at(i), d))
        copy.start()
        nb_copies.append(copy)

    gather_s1.finish()
    for z in range(NZ):
        d_buf[z] = rd[z] * (x_buf[4, z] + natural(s1_full, z))
    for k in range(OWN):
        value = x_buf[4, base + k] + natural(s1_full, base + k) + x_buf[0, base + k]
        put_natural(stage, value, 1, k)
    outs.append(pltpu.make_async_copy(stage.at[1], relaxed.at[1], out_sem.at[1]))
    outs[1].start()
    gather_s2.forward()
    phi(first)
    gather_s2.finish()
    for z in range(NZ):
        d_buf[z] = rd[z] * (x_buf[4, z] + natural(s2_full, z))
    for k in range(OWN):
        value = x_buf[4, base + k] + natural(s2_full, base + k) + x_buf[1, base + k]
        put_natural(stage, value, 2, k)
    outs.append(pltpu.make_async_copy(stage.at[2], relaxed.at[2], out_sem.at[2]))
    outs[2].start()
    phi(first)
    for k in range(OWN):
        value = x_buf[4, base + k] + natural(s3_own, k) + x_buf[2, base + k]
        put_natural(stage, value, 3, k)
    outs.append(pltpu.make_async_copy(stage.at[3], relaxed.at[3], out_sem.at[3]))
    outs[3].start()

    r_copy.wait_recv()
    for k in range(OWN):
        put_natural(r_stage, has_before * r_recv[k], k)
    outs.append(pltpu.make_async_copy(r_stage, residual.at[0], out_sem.at[4]))
    outs[4].start()

    for copy in nb_copies:
        copy.wait_recv()
    row = nb[0]
    for i in range(1, levels):
        row = row + nb[i]
    norm[...] = jnp.broadcast_to(jnp.sum(row, axis=1, keepdims=True), (1, NY))

    for gather in (gather_a, gather_u, gather_s1, gather_s2, gather_e):
        gather.drain()
    for copy in (part_right, part_left, v_own, v_right_late, v_left_late, v_right, v_left, r_copy):
        copy.wait_send()
    for copy in na_copies + nb_copies:
        copy.wait_send()
    for copy in outs:
        copy.wait()


def local(state, source, absorption):
    levels = lax.axis_size("tm") // PLANE
    f32 = jnp.float32
    packed = (NZ, 8, 8, NY)
    any_spec = pl.BlockSpec(memory_space=pl.ANY)
    vm = lambda *shape: pltpu.VMEM(shape, f32)
    dma = lambda *shape: pltpu.SemaphoreType.DMA(shape)
    relaxed, residual, norm = pl.pallas_call(
        kernel,
        out_shape=(
            jax.ShapeDtypeStruct((CF, OWN, NX, NY), f32),
            jax.ShapeDtypeStruct((1, OWN, NX, NY), f32),
            jax.ShapeDtypeStruct((1, NY), f32),
        ),
        in_specs=[any_spec] * 3,
        out_specs=(any_spec, any_spec, pl.BlockSpec(memory_space=pltpu.VMEM)),
        scratch_shapes=[
            vm(NZ, NX, NY), vm(NZ, NX, NY), vm(NZ, NX, NY), vm(NZ, NX, NY),
            vm(OWN, NX, NY), vm(OWN, NX, NY),
            vm(*packed), vm(*packed), vm(*packed), vm(*packed),
            vm(*packed), vm(*packed), vm(*packed), vm(*packed), vm(*packed),
            vm(5, *packed),
            vm(2, 8, 8, NY), vm(2, 8, 8, NY),
            vm(OWN, 8, 8, NY), vm(OWN, 8, 8, NY), vm(OWN, 8, 8, NY),
            vm(CF, OWN, NX, NY), vm(OWN, 8, 8, NY), vm(OWN, NX, NY),
            vm(PLANE, 1, NY), vm(levels, 1, NY),
            dma(6), dma(5), dma(5, 4), dma(5, 4), dma(2), dma(2), dma(5), dma(5),
            dma(1), dma(1), dma(PLANE - 1), dma(PLANE - 1), dma(levels - 1), dma(levels - 1),
        ],
        compiler_params=pltpu.CompilerParams(
            collective_id=0, has_side_effects=True, vmem_limit_bytes=32 * 1024 * 1024
        ),
    )(state, source, absorption)
    return relaxed, residual, norm[0, 0]


def solution(mesh):
    return jax.shard_map(
        local,
        mesh=mesh,
        in_specs=(P("tm", "space", None, None), P("tm", "space", None, None), P("space", None, None)),
        out_specs=(P("tm", "space", None, None), P("tm", "space", None, None), P()),
        check_vma=False,
    )
```

time: 164 us -> 74.2 us (0.45)
  blocking collectives: 80.7 us -> 0 us
  Pallas kernels: 0 us -> 67.2 us
  waiting for transfers between devices: 36 us -> 0 us
  other arithmetic: 21.2 us -> 0 us
  starting transfers between devices: 20.3 us -> 0 us
    pallas_call x0 -> x1, Pallas kernels: none -> 67.2 us  [local(): pl.pallas_call(kernel, out_shape=(jax.ShapeDtypeStruct((CF, OWN, NX, NY),...]
    psum x4 -> x0, blocking collectives: 61.5 us -> none  [by_axis(): value = lax.psum(value, axis)]
    all_to_all x1 -> x0, waiting for transfers between devices: 32.2 us -> none  [sent_to_all(): lax.all_to_all(jnp.broadcast_to(value[None], (count, *value.shape)), axis...]
    all_to_all x2 -> x0, blocking collectives: 19.3 us -> none  [sent_to_all(): lax.all_to_all(jnp.broadcast_to(value[None], (count, *value.shape)), axis...]
    ppermute x2 -> x0, starting transfers between devices: 15.3 us -> none  [shifted(): return lax.ppermute(value, axis, pairs)]
    add x31 -> x0, other arithmetic: 13 us -> none  [the longest x30 12.9 us: step_whole(): field + weight * (rhs - apply_inner(extended, diag_full)) / diag_full]
    all_to_all x1 -> x0, starting transfers between devices: 5 us -> none  [sent_to_all(): lax.all_to_all(jnp.broadcast_to(value[None], (count, *value.shape)), axis...]
    unnamed x0 -> x8, local copies, waits for them, and re-layouts: none -> 4.43 us
  transfers between devices with their start and end apart: 3 -> 0, of which waited for: 3 -> 0; matrix products, arithmetic and copies ran while one was open for 0% -> 0% of each run, Pallas kernels for 0% -> 0%
where the time goes in v1:
time: 74.2 us; the launch traced here: 73.5 us
  Pallas kernels  67.2 us (91%)
  local copies, waits for them, and re-layouts  4.43 us (6%)
  between operations  1.82 us (2%)
    pallas_call x1, Pallas kernels, local(): pl.pallas_call(kernel, out_shape=(jax.ShapeDtypeStruct((CF, OWN, NX, NY),...  67.2 us
    unnamed x8, local copies, waits for them, and re-layouts  4.43 us

profile of v1, /device:TPU:1, one launch (start us, length us, event | category | flops | bytes accessed | tf_op | source)
XLA Modules:
  0.0 73.5 jit_solution(3439923438304807684)
XLA Ops:
  0.6 0.0 copy-start
  0.6 1.0 %copy-done = f32[4,4,64,128]{3,2,1,0:T(8,128)S(1)} copy-done((f32[4,4,64,128]{3,2,1,0:T(8,128)S(1)}, f32[4,4,64,128]{3,2,1,0:T(8,128)}, u32[]{:S(2)}) %copy-start) | copy-done | bytes 524312
  1.7 0.0 copy-start.1
  1.7 1.0 %copy-done.1 = f32[4,4,64,128]{3,2,1,0:T(8,128)S(1)} copy-done((f32[4,4,64,128]{3,2,1,0:T(8,128)S(1)}, f32[4,4,64,128]{3,2,1,0:T(8,128)}, u32[]{:S(2)}) %copy-start.1) | copy-done | bytes 524312
  2.7 0.0 copy-start.2
  2.7 0.9 %copy-done.2 = f32[4,64,128]{2,1,0:T(8,128)S(1)} copy-done((f32[4,64,128]{2,1,0:T(8,128)S(1)}, f32[4,64,128]{2,1,0:T(8,128)}, u32[]{:S(2)}) %copy-start.2) | copy-done | bytes 131096
  3.6 67.2 %shard_map.58 = (f32[4,4,64,128]{3,2,1,0:T(8,128)S(1)}, f32[1,4,64,128]{3,2,1,0:T(8,128)S(1)}, f32[1,128]{1,0:T(1,128)S(1)}) custom-call(f32[4,4,64,128]{3,2,1,0:T(8,128)S(1)} %copy-done, f32[4,4,64,128]{3,2,1,0:T(8,128)S(1)} %copy-done.1, f32[4,64,128]{2,1,0:T(8,128)S(1)} %copy-done.2), custom_call_target="tpu_custom_call" | custom-call | tf_op jit(solution)/shard_map/pallas_call | solution.py:362
  70.9 0.8 %copy.9 = f32[4,4,64,128]{3,2,1,0:T(8,128)} copy(f32[4,4,64,128]{3,2,1,0:T(8,128)S(1)} %get-tuple-element.12) | data formatting | bytes 1048576
  71.6 0.7 copy.10
Async XLA Ops:
  0.6 1.0 %copy-start = (f32[4,4,64,128]{3,2,1,0:T(8,128)S(1)}, f32[4,4,64,128]{3,2,1,0:T(8,128)}, u32[]{:S(2)}) copy-start(f32[4,4,64,128]{3,2,1,0:T(8,128)} %state.1) | copy-start | bytes 1572868
  1.7 1.0 %copy-start.1 = (f32[4,4,64,128]{3,2,1,0:T(8,128)S(1)}, f32[4,4,64,128]{3,2,1,0:T(8,128)}, u32[]{:S(2)}) copy-start(f32[4,4,64,128]{3,2,1,0:T(8,128)} %source.1) | copy-start | bytes 1572868
  2.7 0.9 %copy-start.2 = (f32[4,64,128]{2,1,0:T(8,128)S(1)}, f32[4,64,128]{2,1,0:T(8,128)}, u32[]{:S(2)}) copy-start(f32[4,64,128]{2,1,0:T(8,128)} %absorption.1) | copy-start | bytes 393220

commit v2 on v1

--- a/solution.py
+++ b/solution.py
@@ -16,6 +16,8 @@
 OWN = 4
 SPACES = 4
 PLANE = 8
+READY = 3
+VMEM_BYTES = 67043328
 
 
 def sweep_weights(count):
@@ -47,7 +49,7 @@
     rs_left, rs_right, rv_own, rv_left, rv_right, stage, r_recv, r_stage,
     na, nb,
     local_sem, out_sem, ag_send, ag_recv, rs_send, rs_recv, v_send, v_recv,
-    r_send, r_recv_sem, na_send, na_recv, nb_send, nb_recv,
+    r_send, r_recv_sem, na_send, na_recv, nb_send, nb_recv, ready_sem,
 ):
     c = lax.axis_index("tm")
     d = lax.axis_index("space")
@@ -86,7 +88,7 @@
     peers = [at(c, left), at(c, right)]
     peers += [at(t, s) for t in (after, before) for s in (d, left, right)]
     peers += [at(seat_at(i), d) for i in range(1, PLANE)]
-    peers += [at(level_at(i), d) for i in range(1, levels)]
+    peers += [at(level_at(i), d) for i in (1, levels - 1)]
     for peer in peers:
         pl.semaphore_signal(barrier, inc=1, device_id=peer, device_id_type=MESH)
 
@@ -99,6 +101,14 @@
     def put_natural(ref, value, *index):
         for v in range(8):
             ref[(*index, pl.ds(v, 8, stride=8), slice(None))] = value[v]
+
+    def ready_signal(stage):
+        reach = 2 ** stage
+        for i in (reach, levels - reach):
+            pl.semaphore_signal(ready_sem.at[stage], inc=1, device_id=at(level_at(i), d), device_id_type=MESH)
+
+    def ready_wait(stage):
+        pl.semaphore_wait(ready_sem.at[stage], 2)
 
     class Gather:
         def __init__(self, full, slot):
@@ -167,6 +177,7 @@
     pl.semaphore_wait(barrier, len(peers))
 
     gather_a.start()
+    ready_signal(0)
     for load in loads[1:]:
         load.wait()
     for z in range(NZ):
@@ -174,6 +185,8 @@
     gather_a.forward()
     gather_u.start()
     gather_a.finish()
+    ready_wait(0)
+    ready_signal(1)
     for z in range(NZ):
         inverse = 1.0 / (1.0 + 6.0 * COUPLING + natural(a_full, z))
         rd[z] = inverse
@@ -201,6 +214,9 @@
 
     phi(respond)
     gather_u.forward()
+
+    ready_wait(1)
+    ready_signal(2)
 
     def remote(src, dst, send, recv, target):
         return pltpu.make_async_remote_copy(
@@ -270,6 +286,11 @@
 
     for j in range(CF - 1):
         phi(chain(j))
+        if j == 1:
+            gather_s1.forward()
+            gather_s2.start()
+    gather_s2.forward()
+    ready_wait(2)
 
     squares = []
 
@@ -290,8 +311,9 @@
         na_copies.append(copy)
     r_copy = remote(x_buf.at[3, mine], r_recv, r_send.at[0], r_recv_sem.at[0], at(after, d))
     r_copy.start()
-    gather_s1.forward()
-    gather_s2.start()
+    gather_s1.finish()
+    for z in range(NZ):
+        d_buf[z] = rd[z] * (x_buf[4, z] + natural(s1_full, z))
     for copy in na_copies:
         copy.wait_recv()
     row = na[0]
@@ -304,15 +326,11 @@
         copy.start()
         nb_copies.append(copy)
 
-    gather_s1.finish()
-    for z in range(NZ):
-        d_buf[z] = rd[z] * (x_buf[4, z] + natural(s1_full, z))
     for k in range(OWN):
         value = x_buf[4, base + k] + natural(s1_full, base + k) + x_buf[0, base + k]
         put_natural(stage, value, 1, k)
     outs.append(pltpu.make_async_copy(stage.at[1], relaxed.at[1], out_sem.at[1]))
     outs[1].start()
-    gather_s2.forward()
     phi(first)
     gather_s2.finish()
     for z in range(NZ):
@@ -380,9 +398,10 @@
             vm(PLANE, 1, NY), vm(levels, 1, NY),
             dma(6), dma(5), dma(5, 4), dma(5, 4), dma(2), dma(2), dma(5), dma(5),
             dma(1), dma(1), dma(PLANE - 1), dma(PLANE - 1), dma(levels - 1), dma(levels - 1),
+            pltpu.SemaphoreType.REGULAR((READY,)),
         ],
         compiler_params=pltpu.CompilerParams(
-            collective_id=0, has_side_effects=True, vmem_limit_bytes=32 * 1024 * 1024
+            collective_id=0, has_side_effects=True, vmem_limit_bytes=VMEM_BYTES
         ),
     )(state, source, absorption)
     return relaxed, residual, norm[0, 0]

time: 74.2 us -> 74.4 us (level)
  local copies, waits for them, and re-layouts: 4.43 us -> 2.58 us
  Pallas kernels: 67.2 us -> 69 us
    unnamed x8 -> x6, local copies, waits for them, and re-layouts: 4.43 us -> 2.58 us
    pallas_call x1, Pallas kernels: 67.2 us -> 69 us  [local(): pl.pallas_call(kernel, out_shape=(jax.ShapeDtypeStruct((CF, OWN, NX, NY),...]
where the time goes in v2:
time: 74.4 us; the launch traced here: 73.4 us
  Pallas kernels  69 us (93%)
  local copies, waits for them, and re-layouts  2.58 us (3%)
  between operations  1.81 us (2%)
    pallas_call x1, Pallas kernels, local(): pl.pallas_call(kernel, out_shape=(jax.ShapeDtypeStruct((CF, OWN, NX, NY),...  69 us
    unnamed x6, local copies, waits for them, and re-layouts  2.58 us

profile of v2, /device:TPU:1, one launch (start us, length us, event | category | flops | bytes accessed | tf_op | source)
XLA Modules:
  0.0 73.4 jit_solution(4571201526575388235)
XLA Ops:
  0.6 69.0 %shard_map.58 = (f32[4,4,64,128]{3,2,1,0:T(8,128)}, f32[1,4,64,128]{3,2,1,0:T(8,128)}, f32[1,128]{1,0:T(1,128)}) custom-call(f32[4,4,64,128]{3,2,1,0:T(8,128)} %state.1, f32[4,4,64,128]{3,2,1,0:T(8,128)} %source.1, f32[4,64,128]{2,1,0:T(8,128)} %absorption.1), custom_call_target="tpu_custom_call" | custom-call | tf_op jit(solution)/shard_map/pallas_call | solution.py:380
  69.7 0.0 copy-start
  69.7 1.9 %copy.9 = f32[4,4,64,128]{3,2,1,0:T(8,128)} copy(f32[4,4,64,128]{3,2,1,0:T(8,128)} %get-tuple-element.12) | data formatting | bytes 1048576
  71.6 0.0 copy-done
  71.6 0.0 copy-start.1
  71.6 0.7 copy.10
  72.3 0.0 copy-done.1
Async XLA Ops:
  69.7 1.9 %copy-start = (f32[1,4,64,128]{3,2,1,0:T(8,128)S(1)}, f32[1,4,64,128]{3,2,1,0:T(8,128)}, u32[]{:S(2)}) copy-start(f32[1,4,64,128]{3,2,1,0:T(8,128)} %get-tuple-element.13) | copy-start | bytes 393220
  71.6 0.7 copy-start.1

commit v3 on v1

v3 whole, which is shorter than its diff:
```python
import math

import jax
import jax.numpy as jnp
import numpy as np
from jax import lax
from jax.experimental import pallas as pl
from jax.experimental.pallas import tpu as pltpu
from jax.sharding import PartitionSpec as P

MESH = pl.DeviceIdType.MESH
CF = 4
SWEEPS = 5
COUPLING = 4.0
NZ, NX, NY = 16, 64, 128
OWN = 4
SPACES = 4
PLANE = 8
REACHES = (1, 2, 4, 1)
COLUMNS = 4
ALL = frozenset(range(16))
VMEM_BYTES = 54272 * 1024


def sweep_weights(count):
    spread = 6.0 * COUPLING / (1.0 + 6.0 * COUPLING)
    return [
        1.0 / (1.0 + spread * math.cos(math.pi * (2 * k + 1) / (2 * count))) for k in range(count)
    ]


def coefficients():
    poly = np.zeros(SWEEPS + 1)
    poly[0] = 1.0
    for w in sweep_weights(SWEEPS):
        shifted = np.concatenate([[0.0], poly[:-1]])
        poly = (1.0 - w) * poly + w * shifted
        poly[0] += w
    return [float(c) for c in poly]


COEF = coefficients()
C2 = 0.5 * (COEF[2] + COEF[3])
C4 = 0.5 * (COEF[4] + COEF[5])


def grow(layers):
    return frozenset((z + step) % NZ for z in layers for step in (-1, 0, 1))


def kernel(
    state, source, absorption, relaxed, residual, norm,
    a_full, u_full, s1_full, s2_full, s0_own, s3_own,
    rd, q1, q2, q3, d_buf, l1, l2, l3, l4, v_buf, e_full, x_buf,
    rs_left, rs_right, rv_own, rv_left, rv_right, stage, r_recv, r_stage,
    na, nb,
    local_sem, out_sem, a_send, a_recv, ag_send, ag_recv, rs_send, rs_recv, v_send, v_recv,
    r_send, r_recv_sem, na_send, na_recv, nb_send, nb_recv, ready_sem,
):
    c = lax.axis_index("tm")
    d = lax.axis_index("space")
    tms = lax.axis_size("tm")
    levels = tms // PLANE
    after, before = lax.rem(c + 1, tms), lax.rem(c + tms - 1, tms)
    right, left = lax.rem(d + 1, SPACES), lax.rem(d + SPACES - 1, SPACES)
    plane, seat = c // PLANE, lax.rem(c, PLANE)
    core = lax.rem(c, 2)
    partner = c + 1 - 2 * core

    def at(t, s):
        return {"tm": t, "space": s}

    def seat_at(i):
        return plane * PLANE + lax.rem(seat + i, PLANE)

    def level_at(i):
        return lax.rem(plane + i, levels) * PLANE + seat

    def remote(src, dst, send, recv, target):
        return pltpu.make_async_remote_copy(
            src_ref=src, dst_ref=dst, send_sem=send, recv_sem=recv,
            device_id=target, device_id_type=MESH,
        )

    loads = []
    for i, (src, dst) in enumerate([
        (absorption, a_full.at[pl.ds(0, OWN)]),
        (state.at[0], u_full.at[pl.ds(0, OWN)]),
        (source.at[1], s1_full.at[pl.ds(0, OWN)]),
        (source.at[2], s2_full.at[pl.ds(0, OWN)]),
        (source.at[0], s0_own),
        (source.at[3], s3_own),
    ]):
        copy = pltpu.make_async_copy(src, dst, local_sem.at[i])
        copy.start()
        loads.append(copy)

    barrier = pltpu.get_barrier_semaphore()
    peers = [at(c, left), at(c, right)]
    peers += [at(t, s) for t in (after, before) for s in (d, left, right)]
    peers += [at(seat_at(i), d) for i in range(1, PLANE)]
    peers += [at(level_at(i), d) for i in (1, levels - 1)]
    for peer in peers:
        pl.semaphore_signal(barrier, inc=1, device_id=peer, device_id_type=MESH)

    rows = lax.broadcasted_iota(jnp.int32, (8, NY), 0)
    lanes = lax.broadcasted_iota(jnp.int32, (8, 8, NY), 2)
    joined = [jnp.where(d == SPACES - 1 - b, 0.0, 1.0).astype(jnp.float32) for b in range(SPACES)]

    def natural(ref, *index):
        return jnp.stack([ref[(*index, pl.ds(v, 8, stride=8), slice(None))] for v in range(8)])

    def put_natural(ref, value, *index):
        for v in range(8):
            ref[(*index, pl.ds(v, 8, stride=8), slice(None))] = value[v]

    def ready_signal(number):
        reach = REACHES[number]
        for i in (reach, levels - reach):
            pl.semaphore_signal(ready_sem.at[number], inc=1, device_id=at(level_at(i), d), device_id_type=MESH)

    def ready_wait(number):
        pl.semaphore_wait(ready_sem.at[number], 2)

    class Gather:
        def __init__(self, full, slot):
            self.full, self.slot = full, slot

        def copy(self, src, dst, count, part, target):
            return remote(self.full.at[pl.ds(src, count)], self.full.at[pl.ds(dst, count)],
                          ag_send.at[self.slot, part], ag_recv.at[self.slot, part], at(c, target))

        def start(self):
            self.copies = [self.copy(0, 12, 4, 0, right), self.copy(0, 4, 4, 1, left)]
            self.copies[0].start()
            self.copies[1].start()

        def forward(self):
            self.copies += [self.copy(12, 8, 2, 2, right), self.copy(6, 10, 2, 3, left)]
            self.copies[0].wait_recv()
            self.copies[2].start()
            self.copies[1].wait_recv()
            self.copies[3].start()

        def finish(self):
            self.copies[2].wait_recv()
            self.copies[3].wait_recv()

        def drain(self):
            for copy in self.copies:
                copy.wait_send()

    gather_u, gather_s1, gather_s2 = Gather(u_full, 0), Gather(s1_full, 1), Gather(s2_full, 2)
    gather_e = Gather(e_full, 3)

    half = 2 * core

    def a_copy(src, dst, count, part, target):
        return remote(a_full.at[pl.ds(src, count)], a_full.at[pl.ds(dst, count)],
                      a_send.at[part], a_recv.at[part], target)

    a_right = a_copy(half, 12 + half, 2, 0, at(c, right))
    a_left = a_copy(half, 4 + half, 2, 1, at(c, left))
    a_on_right = a_copy(12 + half, 8 + half, 1, 2, at(c, right))
    a_on_left = a_copy(4 + half + 1, 8 + half + 1, 1, 3, at(c, left))
    a_give_left = a_copy(12 + half, 12 + half, 2, 4, at(partner, d))
    a_give_right = a_copy(4 + half, 4 + half, 2, 5, at(partner, d))
    a_give_first = a_copy(8 + half, 8 + half, 1, 6, at(partner, d))
    a_give_second = a_copy(8 + half + 1, 8 + half + 1, 1, 7, at(partner, d))

    def neighbours(ref, z, have):
        terms = []
        if z in have:
            x = ref[z]
            up = jnp.where(rows == 0, 0.0, pltpu.roll(x[7], 1, 0))
            down = jnp.where(rows == 7, 0.0, pltpu.roll(x[0], 7, 0))
            terms.append(jnp.concatenate([up[None], x[:7]]) + jnp.concatenate([x[1:], down[None]]))
            terms.append(jnp.where(lanes == 0, 0.0, pltpu.roll(x, 1, 2)))
            terms.append(jnp.where(lanes == NY - 1, 0.0, pltpu.roll(x, NY - 1, 2)))
        above, below = (z + 1) % NZ, (z - 1) % NZ
        if above in have:
            terms.append(ref[above] if above % OWN else joined[z // OWN] * ref[above])
        if below in have:
            terms.append(ref[below] if z % OWN else joined[below // OWN] * ref[below])
        total = terms[0]
        for term in terms[1:]:
            total = total + term
        return total

    steps = [(d_buf, l1, q1), (l1, l2, q2), (l2, l3, q1), (l3, l4, q3)]

    def level(number, layers, have, have_d):
        src, dst, factor = steps[number - 1]
        for z in sorted(layers):
            value = factor[z] * neighbours(src, z, have)
            if number % 2 == 0 and z in have_d:
                value = d_buf[z] + value
            dst[z] = value

    def last_step(layers, have, emit):
        for z in sorted(layers):
            value = q1[z] * neighbours(l4, z, have)
            emit(z, l4[z] + value if z in have else value)

    def phi(emit, want=ALL):
        need = [frozenset(want)]
        for _ in range(SWEEPS - 1):
            need.insert(0, grow(need[0]))
        for number in range(1, SWEEPS):
            level(number, need[number - 1], ALL, ALL)
        last_step(want, ALL, emit)

    def invert(layers):
        for z in layers:
            inverse = 1.0 / (1.0 + 6.0 * COUPLING + natural(a_full, z))
            rd[z] = inverse
            q1[z] = COUPLING * inverse
            q2[z] = (COUPLING * C4 / C2) * inverse
            q3[z] = (COUPLING * C2) * inverse

    loads[0].wait()
    pl.semaphore_wait(barrier, len(peers))

    a_right.start()
    a_left.start()
    ready_signal(0)
    for load in loads[1:]:
        load.wait()
    invert(range(4))
    for k in range(OWN):
        d_buf[k] = rd[k] * natural(u_full, k)
    a_right.wait_recv()
    a_on_right.start()
    a_give_left.start()
    a_left.wait_recv()
    a_on_left.start()
    a_give_right.start()
    gather_u.start()
    a_give_left.wait_recv()
    a_give_right.wait_recv()
    invert((4, 5, 6, 7, 12, 13, 14, 15))

    reach = [frozenset(range(OWN))]
    for _ in range(SWEEPS):
        reach.append(grow(reach[-1]))
    for number in range(1, SWEEPS):
        level(number, reach[number], reach[number - 1], reach[0])
    a_on_right.wait_recv()
    a_give_first.start()
    a_on_left.wait_recv()
    a_give_second.start()
    a_give_first.wait_recv()
    a_give_second.wait_recv()
    invert((8, 9, 10, 11))
    for z in ALL - reach[SWEEPS]:
        d_buf[z] = jnp.zeros((8, 8, NY), jnp.float32)

    def scaled(z, x):
        d_buf[z] = rd[z] * x

    last_step(reach[SWEEPS], reach[SWEEPS - 1], scaled)
    for k in range(OWN):
        d_buf[k] = d_buf[k] + rd[k] * natural(s1_full, k)
    ready_wait(0)
    ready_signal(1)
    phi(scaled)
    for k in range(OWN):
        d_buf[k] = d_buf[k] + rd[k] * natural(s2_full, k)
    gather_u.forward()
    phi(scaled)
    for k in range(OWN):
        d_buf[k] = d_buf[k] + rd[k] * natural(s3_own, k)
    ready_wait(1)
    ready_signal(2)

    def respond(z, x):
        v_buf[z] = x

    phi(respond)

    part_right = remote(v_buf.at[pl.ds(8, 2)], rs_left, rs_send.at[0], rs_recv.at[0], at(c, right))
    part_left = remote(v_buf.at[pl.ds(10, 2)], rs_right, rs_send.at[1], rs_recv.at[1], at(c, left))
    part_right.start()
    part_left.start()
    v_own = remote(v_buf.at[pl.ds(0, 4)], rv_own, v_send.at[0], v_recv.at[0], at(after, d))
    v_own.start()
    v_right_late = remote(v_buf.at[pl.ds(6, 2)], rv_left.at[pl.ds(2, 2)],
                          v_send.at[1], v_recv.at[1], at(after, right))
    v_left_late = remote(v_buf.at[pl.ds(12, 2)], rv_right.at[pl.ds(0, 2)],
                         v_send.at[2], v_recv.at[2], at(after, left))
    v_right_late.start()
    v_left_late.start()
    part_right.wait_recv()
    for k in range(2):
        v_buf[4 + k] = v_buf[4 + k] + rs_left[k]
    v_right = remote(v_buf.at[pl.ds(4, 2)], rv_left.at[pl.ds(0, 2)],
                     v_send.at[3], v_recv.at[3], at(after, right))
    v_right.start()
    part_left.wait_recv()
    for k in range(2):
        v_buf[14 + k] = v_buf[14 + k] + rs_right[k]
    v_left = remote(v_buf.at[pl.ds(14, 2)], rv_right.at[pl.ds(2, 2)],
                    v_send.at[4], v_recv.at[4], at(after, left))
    v_left.start()

    gather_u.finish()
    for z in range(NZ):
        d_buf[z] = rd[z] * natural(u_full, z)

    def first(z, x):
        x_buf[4, z] = x

    phi(first)
    ready_wait(2)
    ready_signal(3)

    for copy in (v_own, v_right_late, v_left_late, v_right, v_left):
        copy.wait_recv()
    has_before = jnp.where(c > 0, 1.0, 0.0).astype(jnp.float32)
    for k in range(OWN):
        q = has_before * (rv_own[k] + rv_left[k] + rv_right[k])
        point = q + natural(s0_own, k)
        put_natural(stage, point, 0, k)
        e_full[k] = point - natural(u_full, k)
    gather_e.start()
    outs = [pltpu.make_async_copy(stage.at[0], relaxed.at[0], out_sem.at[0])]
    outs[0].start()
    gather_e.forward()
    gather_s1.start()

    known = ALL - frozenset((8, 9, 10, 11))
    for z in known:
        d_buf[z] = rd[z] * e_full[z]
    inner = [known]
    for number in range(1, SWEEPS):
        inner.append(ALL - grow(ALL - inner[-1]))
        level(number, inner[number], ALL, ALL)
    gather_e.finish()
    for z in ALL - known:
        d_buf[z] = rd[z] * e_full[z]
    for number in range(1, SWEEPS):
        level(number, ALL - inner[number], ALL, ALL)

    def chain(j):
        def emit(z, x):
            x_buf[j, z] = x
            d_buf[z] = rd[z] * x
        return emit

    last_step(ALL, ALL, chain(0))
    phi(chain(1))
    gather_s1.forward()
    gather_s2.start()
    phi(chain(2))
    ready_wait(3)

    squares = []

    def last(z, x):
        if z < OWN:
            x_buf[3, z] = x
        squares.append(x * x)

    phi(last)
    total = squares[0]
    for square in squares[1:]:
        total = total + square
    has_after = jnp.where(c < tms - 1, 1.0, 0.0).astype(jnp.float32)
    na[0] = has_after * jnp.sum(jnp.sum(total, axis=0), axis=0, keepdims=True)
    na_copy = remote(na.at[0], na.at[1], na_send.at[0], na_recv.at[0], at(partner, d))
    na_copy.start()
    r_copy = remote(x_buf.at[3, pl.ds(0, 4)], r_recv, r_send.at[0], r_recv_sem.at[0], at(after, d))
    na_copy.wait_recv()
    nb[0] = na[0] + na[1]
    nb_copies = []
    for i in range(1, levels * COLUMNS):
        target = lax.rem(plane + i // COLUMNS, levels) * PLANE + lax.rem(seat + 2 * (i % COLUMNS), PLANE)
        copy = remote(nb.at[0], nb.at[i], nb_send.at[i - 1], nb_recv.at[i - 1], at(target, d))
        copy.start()
        nb_copies.append(copy)
    r_copy.start()

    gather_s2.forward()
    gather_s1.finish()
    for z in range(NZ):
        d_buf[z] = rd[z] * (x_buf[4, z] + natural(s1_full, z))
    for k in range(OWN):
        value = x_buf[4, k] + natural(s1_full, k) + x_buf[0, k]
        put_natural(stage, value, 1, k)
    outs.append(pltpu.make_async_copy(stage.at[1], relaxed.at[1], out_sem.at[1]))
    outs[1].start()
    near = frozenset(range(OWN))
    for _ in range(SWEEPS):
        near = grow(near)
    phi(first, near)
    gather_s2.finish()
    for z in near:
        d_buf[z] = rd[z] * (x_buf[4, z] + natural(s2_full, z))
    for k in range(OWN):
        value = x_buf[4, k] + natural(s2_full, k) + x_buf[1, k]
        put_natural(stage, value, 2, k)
    outs.append(pltpu.make_async_copy(stage.at[2], relaxed.at[2], out_sem.at[2]))
    outs[2].start()
    phi(first, range(OWN))
    for k in range(OWN):
        value = x_buf[4, k] + natural(s3_own, k) + x_buf[2, k]
        put_natural(stage, value, 3, k)
    outs.append(pltpu.make_async_copy(stage.at[3], relaxed.at[3], out_sem.at[3]))
    outs[3].start()

    r_copy.wait_recv()
    for k in range(OWN):
        put_natural(r_stage, has_before * r_recv[k], k)
    outs.append(pltpu.make_async_copy(r_stage, residual.at[0], out_sem.at[4]))
    outs[4].start()

    for copy in nb_copies:
        copy.wait_recv()
    row = nb[0]
    for i in range(1, levels * COLUMNS):
        row = row + nb[i]
    norm[...] = jnp.broadcast_to(jnp.sum(row, axis=1, keepdims=True), (1, NY))

    for gather in (gather_u, gather_s1, gather_s2, gather_e):
        gather.drain()
    for copy in (a_right, a_left, a_on_right, a_on_left, a_give_left, a_give_right, a_give_first, a_give_second):
        copy.wait_send()
    for copy in (part_right, part_left, v_own, v_right_late, v_left_late, v_right, v_left, r_copy, na_copy):
        copy.wait_send()
    for copy in nb_copies:
        copy.wait_send()
    for copy in outs:
        copy.wait()


def local(state, source, absorption):
    levels = lax.axis_size("tm") // PLANE
    f32 = jnp.float32
    packed = (NZ, 8, 8, NY)
    any_spec = pl.BlockSpec(memory_space=pl.ANY)
    vm = lambda *shape: pltpu.VMEM(shape, f32)
    dma = lambda *shape: pltpu.SemaphoreType.DMA(shape)
    relaxed, residual, norm = pl.pallas_call(
        kernel,
        out_shape=(
            jax.ShapeDtypeStruct((CF, OWN, NX, NY), f32),
            jax.ShapeDtypeStruct((1, OWN, NX, NY), f32),
            jax.ShapeDtypeStruct((1, NY), f32),
        ),
        in_specs=[any_spec] * 3,
        out_specs=(any_spec, any_spec, pl.BlockSpec(memory_space=pltpu.VMEM)),
        scratch_shapes=[
            vm(NZ, NX, NY), vm(NZ, NX, NY), vm(NZ, NX, NY), vm(NZ, NX, NY),
            vm(OWN, NX, NY), vm(OWN, NX, NY),
            vm(*packed), vm(*packed), vm(*packed), vm(*packed),
            vm(*packed), vm(*packed), vm(*packed), vm(*packed), vm(*packed),
            vm(*packed), vm(*packed), vm(5, *packed),
            vm(2, 8, 8, NY), vm(2, 8, 8, NY),
            vm(OWN, 8, 8, NY), vm(OWN, 8, 8, NY), vm(OWN, 8, 8, NY),
            vm(CF, OWN, NX, NY), vm(OWN, 8, 8, NY), vm(OWN, NX, NY),
            vm(2, 1, NY), vm(levels * COLUMNS, 1, NY),
            dma(6), dma(5), dma(8), dma(8), dma(4, 4), dma(4, 4), dma(2), dma(2), dma(5), dma(5),
            dma(1), dma(1), dma(1), dma(1), dma(levels * COLUMNS - 1), dma(levels * COLUMNS - 1),
            pltpu.SemaphoreType.REGULAR((len(REACHES),)),
        ],
        compiler_params=pltpu.CompilerParams(
            collective_id=0, has_side_effects=True, vmem_limit_bytes=VMEM_BYTES
        ),
    )(state, source, absorption)
    return relaxed, residual, norm[0, 0]


def solution(mesh):
    return jax.shard_map(
        local,
        mesh=mesh,
        in_specs=(P("tm", "space", None, None), P("tm", "space", None, None), P("space", None, None)),
        out_specs=(P("tm", "space", None, None), P("tm", "space", None, None), P()),
        check_vma=False,
    )
```

time: 74.2 us -> 65.5 us (0.88)
  Pallas kernels: 67.2 us -> 61 us
  local copies, waits for them, and re-layouts: 4.43 us -> 2.35 us
    pallas_call x1, Pallas kernels: 67.2 us -> 61 us  [local(): pl.pallas_call(kernel, out_shape=(jax.ShapeDtypeStruct((CF, OWN, NX, NY),...]
    unnamed x8 -> x4, local copies, waits for them, and re-layouts: 4.43 us -> 2.35 us
where the time goes in v3:
time: 65.5 us; the launch traced here: 65.2 us
  Pallas kernels  61 us (93%)
  local copies, waits for them, and re-layouts  2.35 us (4%)
  between operations  1.81 us (3%)
    pallas_call x1, Pallas kernels, local(): pl.pallas_call(kernel, out_shape=(jax.ShapeDtypeStruct((CF, OWN, NX, NY),...  61 us
    unnamed x4, local copies, waits for them, and re-layouts  2.35 us

profile of v3, /device:TPU:1, one launch (start us, length us, event | category | flops | bytes accessed | tf_op | source)
XLA Modules:
  0.0 65.2 jit_solution(11580441802124399055)
XLA Ops:
  0.6 0.0 copy-start
  0.6 0.9 %copy-done = f32[4,64,128]{2,1,0:T(8,128)S(1)} copy-done((f32[4,64,128]{2,1,0:T(8,128)S(1)}, f32[4,64,128]{2,1,0:T(8,128)}, u32[]{:S(2)}) %copy-start) | copy-done | bytes 131096
  1.5 61.0 %shard_map.58 = (f32[4,4,64,128]{3,2,1,0:T(8,128)S(1)}, f32[1,4,64,128]{3,2,1,0:T(8,128)S(1)}, f32[1,128]{1,0:T(1,128)S(1)}) custom-call(f32[4,4,64,128]{3,2,1,0:T(8,128)} %state.1, f32[4,4,64,128]{3,2,1,0:T(8,128)} %source.1, f32[4,64,128]{2,1,0:T(8,128)S(1)} %copy-done), custom_call_target="tpu_custom_call" | custom-call | tf_op jit(solution)/shard_map/pallas_call | solution.py:443
  62.6 0.8 %copy.9 = f32[4,4,64,128]{3,2,1,0:T(8,128)} copy(f32[4,4,64,128]{3,2,1,0:T(8,128)S(1)} %get-tuple-element.12) | data formatting | bytes 1048576
  63.4 0.7 %copy.10 = f32[1,4,64,128]{3,2,1,0:T(8,128)} copy(f32[1,4,64,128]{3,2,1,0:T(8,128)S(1)} %get-tuple-element.13) | data formatting | bytes 262144
Async XLA Ops:
  0.6 0.9 %copy-start = (f32[4,64,128]{2,1,0:T(8,128)S(1)}, f32[4,64,128]{2,1,0:T(8,128)}, u32[]{:S(2)}) copy-start(f32[4,64,128]{2,1,0:T(8,128)} %absorption.1) | copy-start | bytes 393220

commit v4 on v3

--- a/solution.py
+++ b/solution.py
@@ -18,6 +18,7 @@
 PLANE = 8
 REACHES = (1, 2, 4, 1)
 COLUMNS = 4
+HALF = 64
 ALL = frozenset(range(16))
 VMEM_BYTES = 54272 * 1024
 
@@ -52,7 +53,7 @@
     state, source, absorption, relaxed, residual, norm,
     a_full, u_full, s1_full, s2_full, s0_own, s3_own,
     rd, q1, q2, q3, d_buf, l1, l2, l3, l4, v_buf, e_full, x_buf,
-    rs_left, rs_right, rv_own, rv_left, rv_right, stage, r_recv, r_stage,
+    loaded, rs_left, rs_right, rv_own, rv_left, rv_right, stage, r_recv, r_stage,
     na, nb,
     local_sem, out_sem, a_send, a_recv, ag_send, ag_recv, rs_send, rs_recv, v_send, v_recv,
     r_send, r_recv_sem, na_send, na_recv, nb_send, nb_recv, ready_sem,
@@ -84,12 +85,12 @@
 
     loads = []
     for i, (src, dst) in enumerate([
-        (absorption, a_full.at[pl.ds(0, OWN)]),
-        (state.at[0], u_full.at[pl.ds(0, OWN)]),
-        (source.at[1], s1_full.at[pl.ds(0, OWN)]),
-        (source.at[2], s2_full.at[pl.ds(0, OWN)]),
-        (source.at[0], s0_own),
-        (source.at[3], s3_own),
+        (absorption, loaded.at[0]),
+        (state.at[0], loaded.at[1]),
+        (source.at[1], loaded.at[2]),
+        (source.at[2], loaded.at[3]),
+        (source.at[0], loaded.at[4]),
+        (source.at[3], loaded.at[5]),
     ]):
         copy = pltpu.make_async_copy(src, dst, local_sem.at[i])
         copy.start()
@@ -104,15 +105,32 @@
         pl.semaphore_signal(barrier, inc=1, device_id=peer, device_id_type=MESH)
 
     rows = lax.broadcasted_iota(jnp.int32, (8, NY), 0)
-    lanes = lax.broadcasted_iota(jnp.int32, (8, 8, NY), 2)
+    lane = lax.broadcasted_iota(jnp.int32, (8, NY), 1)
+    lanes = lax.broadcasted_iota(jnp.int32, (4, 8, NY), 2) % HALF
+    even, lower = lane % 2 == 0, lane < HALF
+    split = 2 * (lane % HALF) + lane // HALF
+    merge = HALF * (lane % 2) + lane // 2
+    inner_up, inner_down = rows != 7, rows != 0
+    edge_up, edge_down = (rows == 7) & (lane >= HALF), (rows == 0) & lower
+
+    def pick(x, index):
+        return jnp.take_along_axis(x, index, axis=1)
     joined = [jnp.where(d == SPACES - 1 - b, 0.0, 1.0).astype(jnp.float32) for b in range(SPACES)]
 
     def natural(ref, *index):
-        return jnp.stack([ref[(*index, pl.ds(v, 8, stride=8), slice(None))] for v in range(8)])
+        tiles = [[], []]
+        for w in range(4):
+            top = ref[(*index, pl.ds(w, 8, stride=4), slice(None))]
+            low = ref[(*index, pl.ds(NX // 2 + w, 8, stride=4), slice(None))]
+            tiles[0].append(pick(jnp.where(even, top, pltpu.roll(low, 1, 1)), split))
+            tiles[1].append(pick(jnp.where(even, pltpu.roll(top, NY - 1, 1), low), split))
+        return jnp.stack(tiles[0] + tiles[1])
 
     def put_natural(ref, value, *index):
-        for v in range(8):
-            ref[(*index, pl.ds(v, 8, stride=8), slice(None))] = value[v]
+        for w in range(4):
+            first, second = pick(value[w], merge), pick(value[4 + w], merge)
+            ref[(*index, pl.ds(w, 8, stride=4), slice(None))] = jnp.where(even, first, pltpu.roll(second, 1, 1))
+            ref[(*index, pl.ds(NX // 2 + w, 8, stride=4), slice(None))] = jnp.where(even, pltpu.roll(first, NY - 1, 1), second)
 
     def ready_signal(number):
         reach = REACHES[number]
@@ -131,23 +149,29 @@
                           ag_send.at[self.slot, part], ag_recv.at[self.slot, part], at(c, target))
 
         def start(self):
-            self.copies = [self.copy(0, 12, 4, 0, right), self.copy(0, 4, 4, 1, left)]
-            self.copies[0].start()
-            self.copies[1].start()
+            self.first = [self.copy(0, 12, 1, 0, right), self.copy(3, 7, 1, 1, left),
+                          self.copy(1, 13, 1, 2, right), self.copy(2, 6, 1, 3, left)]
+            self.rest = [self.copy(2, 14, 2, 4, right), self.copy(0, 4, 2, 5, left)]
+            self.onward = [self.copy(12, 8, 1, 6, right), self.copy(7, 11, 1, 7, left),
+                           self.copy(13, 9, 1, 8, right), self.copy(6, 10, 1, 9, left)]
+            for copy in self.first + self.rest:
+                copy.start()
 
         def forward(self):
-            self.copies += [self.copy(12, 8, 2, 2, right), self.copy(6, 10, 2, 3, left)]
-            self.copies[0].wait_recv()
-            self.copies[2].start()
-            self.copies[1].wait_recv()
-            self.copies[3].start()
+            for came, goes in zip(self.first, self.onward):
+                came.wait_recv()
+                goes.start()
+
+        def middle(self):
+            for copy in self.rest:
+                copy.wait_recv()
 
         def finish(self):
-            self.copies[2].wait_recv()
-            self.copies[3].wait_recv()
+            for copy in self.onward:
+                copy.wait_recv()
 
         def drain(self):
-            for copy in self.copies:
+            for copy in self.first + self.rest + self.onward:
                 copy.wait_send()
 
     gather_u, gather_s1, gather_s2 = Gather(u_full, 0), Gather(s1_full, 1), Gather(s2_full, 2)
@@ -159,8 +183,10 @@
         return remote(a_full.at[pl.ds(src, count)], a_full.at[pl.ds(dst, count)],
                       a_send.at[part], a_recv.at[part], target)
 
-    a_right = a_copy(half, 12 + half, 2, 0, at(c, right))
-    a_left = a_copy(half, 4 + half, 2, 1, at(c, left))
+    a_right = a_copy(half, 12 + half, 1, 0, at(c, right))
+    a_left = a_copy(half + 1, 4 + half + 1, 1, 1, at(c, left))
+    a_right_rest = a_copy(half + 1, 12 + half + 1, 1, 8, at(c, right))
+    a_left_rest = a_copy(half, 4 + half, 1, 9, at(c, left))
     a_on_right = a_copy(12 + half, 8 + half, 1, 2, at(c, right))
     a_on_left = a_copy(4 + half + 1, 8 + half + 1, 1, 3, at(c, left))
     a_give_left = a_copy(12 + half, 12 + half, 2, 4, at(partner, d))
@@ -172,11 +198,21 @@
         terms = []
         if z in have:
             x = ref[z]
-            up = jnp.where(rows == 0, 0.0, pltpu.roll(x[7], 1, 0))
-            down = jnp.where(rows == 7, 0.0, pltpu.roll(x[0], 7, 0))
-            terms.append(jnp.concatenate([up[None], x[:7]]) + jnp.concatenate([x[1:], down[None]]))
-            terms.append(jnp.where(lanes == 0, 0.0, pltpu.roll(x, 1, 2)))
-            terms.append(jnp.where(lanes == NY - 1, 0.0, pltpu.roll(x, NY - 1, 2)))
+            after_x, before_x = [], []
+            for p in range(2):
+                up, down = pltpu.roll(x[4 * p], 7, 0), pltpu.roll(x[4 * p + 3], 1, 0)
+                across = pltpu.roll(jnp.where(edge_up, up, jnp.where(edge_down, down, 0.0)), HALF, 1)
+                up = jnp.where(inner_up, up, across)
+                down = jnp.where(inner_down, down, across)
+                after_x += [x[4 * p + 1:4 * p + 4], up[None]]
+                before_x += [down[None], x[4 * p:4 * p + 3]]
+            terms.append(jnp.concatenate(after_x) + jnp.concatenate(before_x))
+            evens, odds = x[:4], x[4:]
+            terms.append(jnp.concatenate([odds, evens]))
+            terms.append(jnp.concatenate([
+                jnp.where(lanes == 0, 0.0, pltpu.roll(odds, 1, 2)),
+                jnp.where(lanes == HALF - 1, 0.0, pltpu.roll(evens, NY - 1, 2)),
+            ]))
         above, below = (z + 1) % NZ, (z - 1) % NZ
         if above in have:
             terms.append(ref[above] if above % OWN else joined[z // OWN] * ref[above])
@@ -189,16 +225,22 @@
 
     steps = [(d_buf, l1, q1), (l1, l2, q2), (l2, l3, q1), (l3, l4, q3)]
 
+    turn = [0]
+
+    def in_turn(layers):
+        turn[0] += 1
+        return sorted(layers, key=lambda z: (z - turn[0]) % NZ)
+
     def level(number, layers, have, have_d):
         src, dst, factor = steps[number - 1]
-        for z in sorted(layers):
+        for z in in_turn(layers):
             value = factor[z] * neighbours(src, z, have)
             if number % 2 == 0 and z in have_d:
                 value = d_buf[z] + value
             dst[z] = value
 
     def last_step(layers, have, emit):
-        for z in sorted(layers):
+        for z in in_turn(layers):
             value = q1[z] * neighbours(l4, z, have)
             emit(z, l4[z] + value if z in have else value)
 
@@ -212,28 +254,37 @@
 
     def invert(layers):
         for z in layers:
-            inverse = 1.0 / (1.0 + 6.0 * COUPLING + natural(a_full, z))
+            inverse = 1.0 / (1.0 + 6.0 * COUPLING + a_full[z])
             rd[z] = inverse
             q1[z] = COUPLING * inverse
             q2[z] = (COUPLING * C4 / C2) * inverse
             q3[z] = (COUPLING * C2) * inverse
 
-    loads[0].wait()
+    def place(full, number):
+        loads[number].wait()
+        for k in range(OWN):
+            full[k] = natural(loaded, number, k)
+
+    place(a_full, 0)
     pl.semaphore_wait(barrier, len(peers))
 
     a_right.start()
     a_left.start()
+    a_right_rest.start()
+    a_left_rest.start()
     ready_signal(0)
-    for load in loads[1:]:
-        load.wait()
     invert(range(4))
-    for k in range(OWN):
-        d_buf[k] = rd[k] * natural(u_full, k)
+    for full, number in ((u_full, 1), (s1_full, 2), (s2_full, 3), (s0_own, 4), (s3_own, 5)):
+        place(full, number)
+    for k in range(OWN):
+        d_buf[k] = rd[k] * u_full[k]
     a_right.wait_recv()
     a_on_right.start()
-    a_give_left.start()
     a_left.wait_recv()
     a_on_left.start()
+    a_right_rest.wait_recv()
+    a_give_left.start()
+    a_left_rest.wait_recv()
     a_give_right.start()
     gather_u.start()
     a_give_left.wait_recv()
@@ -260,16 +311,16 @@
 
     last_step(reach[SWEEPS], reach[SWEEPS - 1], scaled)
     for k in range(OWN):
-        d_buf[k] = d_buf[k] + rd[k] * natural(s1_full, k)
+        d_buf[k] = d_buf[k] + rd[k] * s1_full[k]
     ready_wait(0)
     ready_signal(1)
     phi(scaled)
     for k in range(OWN):
-        d_buf[k] = d_buf[k] + rd[k] * natural(s2_full, k)
+        d_buf[k] = d_buf[k] + rd[k] * s2_full[k]
     gather_u.forward()
     phi(scaled)
     for k in range(OWN):
-        d_buf[k] = d_buf[k] + rd[k] * natural(s3_own, k)
+        d_buf[k] = d_buf[k] + rd[k] * s3_own[k]
     ready_wait(1)
     ready_signal(2)
 
@@ -278,34 +329,34 @@
 
     phi(respond)
 
-    part_right = remote(v_buf.at[pl.ds(8, 2)], rs_left, rs_send.at[0], rs_recv.at[0], at(c, right))
-    part_left = remote(v_buf.at[pl.ds(10, 2)], rs_right, rs_send.at[1], rs_recv.at[1], at(c, left))
-    part_right.start()
-    part_left.start()
-    v_own = remote(v_buf.at[pl.ds(0, 4)], rv_own, v_send.at[0], v_recv.at[0], at(after, d))
-    v_own.start()
-    v_right_late = remote(v_buf.at[pl.ds(6, 2)], rv_left.at[pl.ds(2, 2)],
-                          v_send.at[1], v_recv.at[1], at(after, right))
-    v_left_late = remote(v_buf.at[pl.ds(12, 2)], rv_right.at[pl.ds(0, 2)],
-                         v_send.at[2], v_recv.at[2], at(after, left))
-    v_right_late.start()
-    v_left_late.start()
-    part_right.wait_recv()
+    parts = []
     for k in range(2):
-        v_buf[4 + k] = v_buf[4 + k] + rs_left[k]
-    v_right = remote(v_buf.at[pl.ds(4, 2)], rv_left.at[pl.ds(0, 2)],
-                     v_send.at[3], v_recv.at[3], at(after, right))
-    v_right.start()
-    part_left.wait_recv()
-    for k in range(2):
-        v_buf[14 + k] = v_buf[14 + k] + rs_right[k]
-    v_left = remote(v_buf.at[pl.ds(14, 2)], rv_right.at[pl.ds(2, 2)],
-                    v_send.at[4], v_recv.at[4], at(after, left))
-    v_left.start()
-
+        parts.append((remote(v_buf.at[pl.ds(8 + k, 1)], rs_left.at[pl.ds(k, 1)],
+                             rs_send.at[2 * k], rs_recv.at[2 * k], at(c, right)), 4 + k, rs_left, k))
+        parts.append((remote(v_buf.at[pl.ds(10 + k, 1)], rs_right.at[pl.ds(k, 1)],
+                             rs_send.at[2 * k + 1], rs_recv.at[2 * k + 1], at(c, left)), 14 + k, rs_right, k))
+    for part in parts:
+        part[0].start()
+    v_copies = [
+        remote(v_buf.at[pl.ds(0, 4)], rv_own, v_send.at[0], v_recv.at[0], at(after, d)),
+        remote(v_buf.at[pl.ds(6, 2)], rv_left.at[pl.ds(2, 2)], v_send.at[1], v_recv.at[1], at(after, right)),
+        remote(v_buf.at[pl.ds(12, 2)], rv_right.at[pl.ds(0, 2)], v_send.at[2], v_recv.at[2], at(after, left)),
+    ]
+    for copy in v_copies:
+        copy.start()
+    for i, (part, layer, came, k) in enumerate(parts):
+        part.wait_recv()
+        v_buf[layer] = v_buf[layer] + came[k]
+        dst, target = (rv_left, right) if came is rs_left else (rv_right, left)
+        copy = remote(v_buf.at[pl.ds(layer, 1)], dst.at[pl.ds(layer - (4 if came is rs_left else 12), 1)],
+                      v_send.at[3 + i], v_recv.at[3 + i], at(after, target))
+        copy.start()
+        v_copies.append(copy)
+
+    gather_u.middle()
     gather_u.finish()
     for z in range(NZ):
-        d_buf[z] = rd[z] * natural(u_full, z)
+        d_buf[z] = rd[z] * u_full[z]
 
     def first(z, x):
         x_buf[4, z] = x
@@ -314,19 +365,20 @@
     ready_wait(2)
     ready_signal(3)
 
-    for copy in (v_own, v_right_late, v_left_late, v_right, v_left):
+    for copy in v_copies:
         copy.wait_recv()
     has_before = jnp.where(c > 0, 1.0, 0.0).astype(jnp.float32)
     for k in range(OWN):
         q = has_before * (rv_own[k] + rv_left[k] + rv_right[k])
-        point = q + natural(s0_own, k)
+        point = q + s0_own[k]
         put_natural(stage, point, 0, k)
-        e_full[k] = point - natural(u_full, k)
+        e_full[k] = point - u_full[k]
     gather_e.start()
     outs = [pltpu.make_async_copy(stage.at[0], relaxed.at[0], out_sem.at[0])]
     outs[0].start()
     gather_e.forward()
     gather_s1.start()
+    gather_e.middle()
 
     known = ALL - frozenset((8, 9, 10, 11))
     for z in known:
@@ -381,11 +433,12 @@
     r_copy.start()
 
     gather_s2.forward()
+    gather_s1.middle()
     gather_s1.finish()
     for z in range(NZ):
-        d_buf[z] = rd[z] * (x_buf[4, z] + natural(s1_full, z))
-    for k in range(OWN):
-        value = x_buf[4, k] + natural(s1_full, k) + x_buf[0, k]
+        d_buf[z] = rd[z] * (x_buf[4, z] + s1_full[z])
+    for k in range(OWN):
+        value = x_buf[4, k] + s1_full[k] + x_buf[0, k]
         put_natural(stage, value, 1, k)
     outs.append(pltpu.make_async_copy(stage.at[1], relaxed.at[1], out_sem.at[1]))
     outs[1].start()
@@ -393,17 +446,18 @@
     for _ in range(SWEEPS):
         near = grow(near)
     phi(first, near)
+    gather_s2.middle()
     gather_s2.finish()
     for z in near:
-        d_buf[z] = rd[z] * (x_buf[4, z] + natural(s2_full, z))
-    for k in range(OWN):
-        value = x_buf[4, k] + natural(s2_full, k) + x_buf[1, k]
+        d_buf[z] = rd[z] * (x_buf[4, z] + s2_full[z])
+    for k in range(OWN):
+        value = x_buf[4, k] + s2_full[k] + x_buf[1, k]
         put_natural(stage, value, 2, k)
     outs.append(pltpu.make_async_copy(stage.at[2], relaxed.at[2], out_sem.at[2]))
     outs[2].start()
     phi(first, range(OWN))
     for k in range(OWN):
-        value = x_buf[4, k] + natural(s3_own, k) + x_buf[2, k]
+        value = x_buf[4, k] + s3_own[k] + x_buf[2, k]
         put_natural(stage, value, 3, k)
     outs.append(pltpu.make_async_copy(stage.at[3], relaxed.at[3], out_sem.at[3]))
     outs[3].start()
@@ -423,9 +477,9 @@
 
     for gather in (gather_u, gather_s1, gather_s2, gather_e):
         gather.drain()
-    for copy in (a_right, a_left, a_on_right, a_on_left, a_give_left, a_give_right, a_give_first, a_give_second):
+    for copy in (a_right_rest, a_left_rest, a_right, a_left, a_on_right, a_on_left, a_give_left, a_give_right, a_give_first, a_give_second):
         copy.wait_send()
-    for copy in (part_right, part_left, v_own, v_right_late, v_left_late, v_right, v_left, r_copy, na_copy):
+    for copy in [part[0] for part in parts] + v_copies + [r_copy, na_copy]:
         copy.wait_send()
     for copy in nb_copies:
         copy.wait_send()
@@ -450,16 +504,16 @@
         in_specs=[any_spec] * 3,
         out_specs=(any_spec, any_spec, pl.BlockSpec(memory_space=pltpu.VMEM)),
         scratch_shapes=[
-            vm(NZ, NX, NY), vm(NZ, NX, NY), vm(NZ, NX, NY), vm(NZ, NX, NY),
-            vm(OWN, NX, NY), vm(OWN, NX, NY),
+            vm(*packed), vm(*packed), vm(*packed), vm(*packed),
+            vm(OWN, 8, 8, NY), vm(OWN, 8, 8, NY),
             vm(*packed), vm(*packed), vm(*packed), vm(*packed),
             vm(*packed), vm(*packed), vm(*packed), vm(*packed), vm(*packed),
             vm(*packed), vm(*packed), vm(5, *packed),
-            vm(2, 8, 8, NY), vm(2, 8, 8, NY),
+            vm(6, OWN, NX, NY), vm(2, 8, 8, NY), vm(2, 8, 8, NY),
             vm(OWN, 8, 8, NY), vm(OWN, 8, 8, NY), vm(OWN, 8, 8, NY),
             vm(CF, OWN, NX, NY), vm(OWN, 8, 8, NY), vm(OWN, NX, NY),
             vm(2, 1, NY), vm(levels * COLUMNS, 1, NY),
-            dma(6), dma(5), dma(8), dma(8), dma(4, 4), dma(4, 4), dma(2), dma(2), dma(5), dma(5),
+            dma(6), dma(5), dma(10), dma(10), dma(4, 10), dma(4, 10), dma(4), dma(4), dma(7), dma(7),
             dma(1), dma(1), dma(1), dma(1), dma(levels * COLUMNS - 1), dma(levels * COLUMNS - 1),
             pltpu.SemaphoreType.REGULAR((len(REACHES),)),
         ],

time: 65.5 us -> 61.2 us (0.934)
  Pallas kernels: 61 us -> 56.4 us
    pallas_call x1, Pallas kernels: 61 us -> 56.4 us  [local(): pl.pallas_call(kernel, out_shape=(jax.ShapeDtypeStruct((CF, OWN, NX, NY),...]
where the time goes in v4:
time: 61.2 us; the launch traced here: 60.6 us
  Pallas kernels  56.4 us (92%)
  local copies, waits for them, and re-layouts  2.35 us (4%)
  between operations  1.81 us (3%)
    pallas_call x1, Pallas kernels, local(): pl.pallas_call(kernel, out_shape=(jax.ShapeDtypeStruct((CF, OWN, NX, NY),...  56.4 us
    unnamed x4, local copies, waits for them, and re-layouts  2.35 us

profile of v4, /device:TPU:1, one launch (start us, length us, event | category | flops | bytes accessed | tf_op | source)
XLA Modules:
  0.0 60.6 jit_solution(14991220883825036203)
XLA Ops:
  0.6 0.0 copy-start
  0.6 0.9 %copy-done = f32[4,64,128]{2,1,0:T(8,128)S(1)} copy-done((f32[4,64,128]{2,1,0:T(8,128)S(1)}, f32[4,64,128]{2,1,0:T(8,128)}, u32[]{:S(2)}) %copy-start) | copy-done | bytes 131096
  1.5 56.4 %shard_map.58 = (f32[4,4,64,128]{3,2,1,0:T(8,128)S(1)}, f32[1,4,64,128]{3,2,1,0:T(8,128)S(1)}, f32[1,128]{1,0:T(1,128)S(1)}) custom-call(f32[4,4,64,128]{3,2,1,0:T(8,128)} %state.1, f32[4,4,64,128]{3,2,1,0:T(8,128)} %source.1, f32[4,64,128]{2,1,0:T(8,128)S(1)} %copy-done), custom_call_target="tpu_custom_call" | custom-call | tf_op jit(solution)/shard_map/pallas_call | solution.py:497
  58.0 0.8 %copy.9 = f32[4,4,64,128]{3,2,1,0:T(8,128)} copy(f32[4,4,64,128]{3,2,1,0:T(8,128)S(1)} %get-tuple-element.12) | data formatting | bytes 1048576
  58.8 0.7 %copy.10 = f32[1,4,64,128]{3,2,1,0:T(8,128)} copy(f32[1,4,64,128]{3,2,1,0:T(8,128)S(1)} %get-tuple-element.13) | data formatting | bytes 262144
Async XLA Ops:
  0.6 0.9 %copy-start = (f32[4,64,128]{2,1,0:T(8,128)S(1)}, f32[4,64,128]{2,1,0:T(8,128)}, u32[]{:S(2)}) copy-start(f32[4,64,128]{2,1,0:T(8,128)} %absorption.1) | copy-start | bytes 393220

commit v5 on v4

--- a/solution.py
+++ b/solution.py
@@ -20,7 +20,7 @@
 COLUMNS = 4
 HALF = 64
 ALL = frozenset(range(16))
-VMEM_BYTES = 54272 * 1024
+VMEM_BYTES = 48 * 1024 * 1024
 
 
 def sweep_weights(count):
@@ -239,18 +239,18 @@
                 value = d_buf[z] + value
             dst[z] = value
 
-    def last_step(layers, have, emit):
-        for z in in_turn(layers):
+    def last_step(layers, have, emit, order=None):
+        for z in order or in_turn(layers):
             value = q1[z] * neighbours(l4, z, have)
             emit(z, l4[z] + value if z in have else value)
 
-    def phi(emit, want=ALL):
+    def phi(emit, want=ALL, order=None):
         need = [frozenset(want)]
         for _ in range(SWEEPS - 1):
             need.insert(0, grow(need[0]))
         for number in range(1, SWEEPS):
             level(number, need[number - 1], ALL, ALL)
-        last_step(want, ALL, emit)
+        last_step(want, ALL, emit, order)
 
     def invert(layers):
         for z in layers:
@@ -324,19 +324,20 @@
     ready_wait(1)
     ready_signal(2)
 
-    def respond(z, x):
-        v_buf[z] = x
-
-    phi(respond)
-
     parts = []
     for k in range(2):
         parts.append((remote(v_buf.at[pl.ds(8 + k, 1)], rs_left.at[pl.ds(k, 1)],
                              rs_send.at[2 * k], rs_recv.at[2 * k], at(c, right)), 4 + k, rs_left, k))
         parts.append((remote(v_buf.at[pl.ds(10 + k, 1)], rs_right.at[pl.ds(k, 1)],
                              rs_send.at[2 * k + 1], rs_recv.at[2 * k + 1], at(c, left)), 14 + k, rs_right, k))
-    for part in parts:
-        part[0].start()
+
+    def respond(z, x):
+        v_buf[z] = x
+        if z == 11:
+            for part in parts:
+                part[0].start()
+
+    phi(respond, ALL, (8, 9, 10, 11, 6, 7, 12, 13, 0, 1, 2, 3, 4, 5, 14, 15))
     v_copies = [
         remote(v_buf.at[pl.ds(0, 4)], rv_own, v_send.at[0], v_recv.at[0], at(after, d)),
         remote(v_buf.at[pl.ds(6, 2)], rv_left.at[pl.ds(2, 2)], v_send.at[1], v_recv.at[1], at(after, right)),
@@ -370,10 +371,11 @@
     has_before = jnp.where(c > 0, 1.0, 0.0).astype(jnp.float32)
     for k in range(OWN):
         q = has_before * (rv_own[k] + rv_left[k] + rv_right[k])
-        point = q + s0_own[k]
-        put_natural(stage, point, 0, k)
-        e_full[k] = point - u_full[k]
+        e_full[k] = q + s0_own[k] - u_full[k]
     gather_e.start()
+    for k in range(OWN):
+        q = has_before * (rv_own[k] + rv_left[k] + rv_right[k])
+        put_natural(stage, q + s0_own[k], 0, k)
     outs = [pltpu.make_async_copy(stage.at[0], relaxed.at[0], out_sem.at[0])]
     outs[0].start()
     gather_e.forward()
@@ -425,7 +427,8 @@
     na_copy.wait_recv()
     nb[0] = na[0] + na[1]
     nb_copies = []
-    for i in range(1, levels * COLUMNS):
+    farthest_first = sorted(range(1, levels * COLUMNS), key=lambda i: -min(i // COLUMNS, levels - i // COLUMNS))
+    for i in farthest_first:
         target = lax.rem(plane + i // COLUMNS, levels) * PLANE + lax.rem(seat + 2 * (i % COLUMNS), PLANE)
         copy = remote(nb.at[0], nb.at[i], nb_send.at[i - 1], nb_recv.at[i - 1], at(target, d))
         copy.start()
@@ -484,6 +487,17 @@
     for copy in nb_copies:
         copy.wait_send()
     for copy in outs:
+        copy.wait()
+
+
+def write_out(relaxed, residual, relaxed_out, residual_out, sem):
+    copies = [
+        pltpu.make_async_copy(relaxed, relaxed_out, sem.at[0]),
+        pltpu.make_async_copy(residual, residual_out, sem.at[1]),
+    ]
+    for copy in copies:
+        copy.start()
+    for copy in copies:
         copy.wait()
 
 
@@ -520,7 +534,15 @@
         compiler_params=pltpu.CompilerParams(
             collective_id=0, has_side_effects=True, vmem_limit_bytes=VMEM_BYTES
         ),
-    )(state, source, absorption)
+    )(*(pltpu.with_memory_space_constraint(array, pltpu.HBM) for array in (state, source, absorption)))
+    relaxed, residual = pl.pallas_call(
+        write_out,
+        out_shape=(jax.ShapeDtypeStruct(relaxed.shape, f32), jax.ShapeDtypeStruct(residual.shape, f32)),
+        in_specs=[any_spec] * 2,
+        out_specs=(any_spec, any_spec),
+        scratch_shapes=[dma(2)],
+        compiler_params=pltpu.CompilerParams(vmem_limit_bytes=1024 * 1024),
+    )(relaxed, residual)
     return relaxed, residual, norm[0, 0]
 
 

time: 61.2 us -> 58.8 us (0.961)
  local copies, waits for them, and re-layouts: 2.35 us -> 0 us
    unnamed x4 -> x0, local copies, waits for them, and re-layouts: 2.35 us -> none
    pallas_call x0 -> x1, Pallas kernels: none -> 0.85 us  [local(): pl.pallas_call(write_out, out_shape=(jax.ShapeDtypeStruct(relaxed.shape,...]
where the time goes in v5:
time: 58.8 us; the launch traced here: 58.7 us
  Pallas kernels  56.9 us (97%)
  between operations  1.8 us (3%)
    pallas_call x1, Pallas kernels, local(): pl.pallas_call(kernel, out_shape=(jax.ShapeDtypeStruct((CF, OWN, NX, NY),...  56 us

profile of v5, /device:TPU:1, one launch (start us, length us, event | category | flops | bytes accessed | tf_op | source)
XLA Modules:
  0.0 58.7 jit_solution(130470862970662849)
XLA Ops:
  0.6 56.0 %shard_map.58 = (f32[4,4,64,128]{3,2,1,0:T(8,128)S(1)}, f32[1,4,64,128]{3,2,1,0:T(8,128)S(1)}, f32[1,128]{1,0:T(1,128)S(1)}) custom-call(f32[4,4,64,128]{3,2,1,0:T(8,128)} %state.1, f32[4,4,64,128]{3,2,1,0:T(8,128)} %source.1, f32[4,64,128]{2,1,0:T(8,128)} %absorption.1), custom_call_target="tpu_custom_call" | custom-call | tf_op jit(solution)/shard_map/pallas_call | solution.py:511
  56.7 0.8 %shard_map.59 = (f32[4,4,64,128]{3,2,1,0:T(8,128)}, f32[1,4,64,128]{3,2,1,0:T(8,128)}) custom-call(f32[4,4,64,128]{3,2,1,0:T(8,128)S(1)} %get-tuple-element.8.relaxed, f32[1,4,64,128]{3,2,1,0:T(8,128)S(1)} %get-tuple-element.9.residual), custom_call_target="tpu_custom_call" | custom-call | tf_op jit(solution)/shard_map/pallas_call | solution.py:538

commit v6 on v5

--- a/solution.py
+++ b/solution.py
@@ -53,7 +53,7 @@
     state, source, absorption, relaxed, residual, norm,
     a_full, u_full, s1_full, s2_full, s0_own, s3_own,
     rd, q1, q2, q3, d_buf, l1, l2, l3, l4, v_buf, e_full, x_buf,
-    loaded, rs_left, rs_right, rv_own, rv_left, rv_right, stage, r_recv, r_stage,
+    loaded, point_buf, rs_left, rs_right, rv_own, rv_left, rv_right, stage, r_recv, r_stage,
     na, nb,
     local_sem, out_sem, a_send, a_recv, ag_send, ag_recv, rs_send, rs_recv, v_send, v_recv,
     r_send, r_recv_sem, na_send, na_recv, nb_send, nb_recv, ready_sem,
@@ -148,12 +148,15 @@
             return remote(self.full.at[pl.ds(src, count)], self.full.at[pl.ds(dst, count)],
                           ag_send.at[self.slot, part], ag_recv.at[self.slot, part], at(c, target))
 
+        def prepare(self):
+            self.first = [self.copy(0, 12, 1, 0, right), self.copy(2, 6, 1, 1, left),
+                          self.copy(1, 13, 1, 2, right), self.copy(3, 7, 1, 3, left)]
+            self.rest = [self.copy(2, 14, 2, 4, right), self.copy(0, 4, 2, 5, left)]
+            self.onward = [self.copy(12, 8, 1, 6, right), self.copy(6, 10, 1, 7, left),
+                           self.copy(13, 9, 1, 8, right), self.copy(7, 11, 1, 9, left)]
+
         def start(self):
-            self.first = [self.copy(0, 12, 1, 0, right), self.copy(3, 7, 1, 1, left),
-                          self.copy(1, 13, 1, 2, right), self.copy(2, 6, 1, 3, left)]
-            self.rest = [self.copy(2, 14, 2, 4, right), self.copy(0, 4, 2, 5, left)]
-            self.onward = [self.copy(12, 8, 1, 6, right), self.copy(7, 11, 1, 7, left),
-                           self.copy(13, 9, 1, 8, right), self.copy(6, 10, 1, 9, left)]
+            self.prepare()
             for copy in self.first + self.rest:
                 copy.start()
 
@@ -177,22 +180,13 @@
     gather_u, gather_s1, gather_s2 = Gather(u_full, 0), Gather(s1_full, 1), Gather(s2_full, 2)
     gather_e = Gather(e_full, 3)
 
-    half = 2 * core
-
-    def a_copy(src, dst, count, part, target):
-        return remote(a_full.at[pl.ds(src, count)], a_full.at[pl.ds(dst, count)],
-                      a_send.at[part], a_recv.at[part], target)
-
-    a_right = a_copy(half, 12 + half, 1, 0, at(c, right))
-    a_left = a_copy(half + 1, 4 + half + 1, 1, 1, at(c, left))
-    a_right_rest = a_copy(half + 1, 12 + half + 1, 1, 8, at(c, right))
-    a_left_rest = a_copy(half, 4 + half, 1, 9, at(c, left))
-    a_on_right = a_copy(12 + half, 8 + half, 1, 2, at(c, right))
-    a_on_left = a_copy(4 + half + 1, 8 + half + 1, 1, 3, at(c, left))
-    a_give_left = a_copy(12 + half, 12 + half, 2, 4, at(partner, d))
-    a_give_right = a_copy(4 + half, 4 + half, 2, 5, at(partner, d))
-    a_give_first = a_copy(8 + half, 8 + half, 1, 6, at(partner, d))
-    a_give_second = a_copy(8 + half + 1, 8 + half + 1, 1, 7, at(partner, d))
+    gather_a = Gather(a_full, 4)
+
+    def a_give(first, count, part):
+        return remote(a_full.at[pl.ds(first, count)], a_full.at[pl.ds(first, count)],
+                      a_send.at[part], a_recv.at[part], at(partner, d))
+
+    a_gives = [a_give(4, 4, 0), a_give(12, 4, 1), a_give(8, 4, 2)]
 
     def neighbours(ref, z, have):
         terms = []
@@ -268,27 +262,33 @@
     place(a_full, 0)
     pl.semaphore_wait(barrier, len(peers))
 
-    a_right.start()
-    a_left.start()
-    a_right_rest.start()
-    a_left_rest.start()
+    gather_a.prepare()
+
+    @pl.when(core == 1)
+    def _():
+        for copy in gather_a.first + gather_a.rest:
+            copy.start()
+
     ready_signal(0)
     invert(range(4))
     for full, number in ((u_full, 1), (s1_full, 2), (s2_full, 3), (s0_own, 4), (s3_own, 5)):
         place(full, number)
     for k in range(OWN):
         d_buf[k] = rd[k] * u_full[k]
-    a_right.wait_recv()
-    a_on_right.start()
-    a_left.wait_recv()
-    a_on_left.start()
-    a_right_rest.wait_recv()
-    a_give_left.start()
-    a_left_rest.wait_recv()
-    a_give_right.start()
+
+    @pl.when(core == 1)
+    def _():
+        gather_a.forward()
+        gather_a.middle()
+        a_gives[0].start()
+        a_gives[1].start()
+
+    @pl.when(core == 0)
+    def _():
+        a_gives[0].wait_recv()
+        a_gives[1].wait_recv()
+
     gather_u.start()
-    a_give_left.wait_recv()
-    a_give_right.wait_recv()
     invert((4, 5, 6, 7, 12, 13, 14, 15))
 
     reach = [frozenset(range(OWN))]
@@ -296,25 +296,38 @@
         reach.append(grow(reach[-1]))
     for number in range(1, SWEEPS):
         level(number, reach[number], reach[number - 1], reach[0])
-    a_on_right.wait_recv()
-    a_give_first.start()
-    a_on_left.wait_recv()
-    a_give_second.start()
-    a_give_first.wait_recv()
-    a_give_second.wait_recv()
-    invert((8, 9, 10, 11))
-    for z in ALL - reach[SWEEPS]:
-        d_buf[z] = jnp.zeros((8, 8, NY), jnp.float32)
 
     def scaled(z, x):
         d_buf[z] = rd[z] * x
 
-    last_step(reach[SWEEPS], reach[SWEEPS - 1], scaled)
+    known = ALL - frozenset((8, 9, 10, 11))
+    inner = [known]
+    for _ in range(1, SWEEPS):
+        inner.append(ALL - grow(ALL - inner[-1]))
+    last_step(known, reach[SWEEPS - 1], scaled)
     for k in range(OWN):
         d_buf[k] = d_buf[k] + rd[k] * s1_full[k]
+    for number in range(1, SWEEPS):
+        level(number, inner[number], ALL, ALL)
+
+    @pl.when(core == 1)
+    def _():
+        gather_a.finish()
+        a_gives[2].start()
+
+    @pl.when(core == 0)
+    def _():
+        a_gives[2].wait_recv()
+
     ready_wait(0)
     ready_signal(1)
-    phi(scaled)
+    invert((8, 9, 10, 11))
+    for z in (9, 10):
+        d_buf[z] = jnp.zeros((8, 8, NY), jnp.float32)
+    last_step((8, 11), reach[SWEEPS - 1], scaled)
+    for number in range(1, SWEEPS):
+        level(number, ALL - inner[number], ALL, ALL)
+    last_step(ALL, ALL, scaled)
     for k in range(OWN):
         d_buf[k] = d_buf[k] + rd[k] * s2_full[k]
     gather_u.forward()
@@ -366,28 +379,31 @@
     ready_wait(2)
     ready_signal(3)
 
-    for copy in v_copies:
+    for copy in v_copies[:3]:
         copy.wait_recv()
     has_before = jnp.where(c > 0, 1.0, 0.0).astype(jnp.float32)
-    for k in range(OWN):
-        q = has_before * (rv_own[k] + rv_left[k] + rv_right[k])
-        e_full[k] = q + s0_own[k] - u_full[k]
-    gather_e.start()
-    for k in range(OWN):
-        q = has_before * (rv_own[k] + rv_left[k] + rv_right[k])
-        put_natural(stage, q + s0_own[k], 0, k)
+    gather_e.prepare()
+    for k in range(2):
+        for copy in v_copies[3 + 2 * k:5 + 2 * k]:
+            copy.wait_recv()
+        for layer in (k, 2 + k):
+            point_buf[layer] = has_before * (rv_own[layer] + rv_left[layer] + rv_right[layer]) + s0_own[layer]
+            e_full[layer] = point_buf[layer] - u_full[layer]
+        for copy in gather_e.first[2 * k:2 * k + 2]:
+            copy.start()
+    for copy in gather_e.rest:
+        copy.start()
+    for k in range(OWN):
+        put_natural(stage, point_buf[k], 0, k)
     outs = [pltpu.make_async_copy(stage.at[0], relaxed.at[0], out_sem.at[0])]
     outs[0].start()
     gather_e.forward()
     gather_s1.start()
     gather_e.middle()
 
-    known = ALL - frozenset((8, 9, 10, 11))
     for z in known:
         d_buf[z] = rd[z] * e_full[z]
-    inner = [known]
     for number in range(1, SWEEPS):
-        inner.append(ALL - grow(ALL - inner[-1]))
         level(number, inner[number], ALL, ALL)
     gather_e.finish()
     for z in ALL - known:
@@ -433,7 +449,6 @@
         copy = remote(nb.at[0], nb.at[i], nb_send.at[i - 1], nb_recv.at[i - 1], at(target, d))
         copy.start()
         nb_copies.append(copy)
-    r_copy.start()
 
     gather_s2.forward()
     gather_s1.middle()
@@ -449,6 +464,7 @@
     for _ in range(SWEEPS):
         near = grow(near)
     phi(first, near)
+    r_copy.start()
     gather_s2.middle()
     gather_s2.finish()
     for z in near:
@@ -480,8 +496,13 @@
 
     for gather in (gather_u, gather_s1, gather_s2, gather_e):
         gather.drain()
-    for copy in (a_right_rest, a_left_rest, a_right, a_left, a_on_right, a_on_left, a_give_left, a_give_right, a_give_first, a_give_second):
-        copy.wait_send()
+
+    @pl.when(core == 1)
+    def _():
+        gather_a.drain()
+        for copy in a_gives:
+            copy.wait_send()
+
     for copy in [part[0] for part in parts] + v_copies + [r_copy, na_copy]:
         copy.wait_send()
     for copy in nb_copies:
@@ -523,11 +544,11 @@
             vm(*packed), vm(*packed), vm(*packed), vm(*packed),
             vm(*packed), vm(*packed), vm(*packed), vm(*packed), vm(*packed),
             vm(*packed), vm(*packed), vm(5, *packed),
-            vm(6, OWN, NX, NY), vm(2, 8, 8, NY), vm(2, 8, 8, NY),
+            vm(6, OWN, NX, NY), vm(OWN, 8, 8, NY), vm(2, 8, 8, NY), vm(2, 8, 8, NY),
             vm(OWN, 8, 8, NY), vm(OWN, 8, 8, NY), vm(OWN, 8, 8, NY),
             vm(CF, OWN, NX, NY), vm(OWN, 8, 8, NY), vm(OWN, NX, NY),
             vm(2, 1, NY), vm(levels * COLUMNS, 1, NY),
-            dma(6), dma(5), dma(10), dma(10), dma(4, 10), dma(4, 10), dma(4), dma(4), dma(7), dma(7),
+            dma(6), dma(5), dma(3), dma(3), dma(5, 10), dma(5, 10), dma(4), dma(4), dma(7), dma(7),
             dma(1), dma(1), dma(1), dma(1), dma(levels * COLUMNS - 1), dma(levels * COLUMNS - 1),
             pltpu.SemaphoreType.REGULAR((len(REACHES),)),
         ],

time: 58.8 us -> 57 us (0.969)
  Pallas kernels: 56.9 us -> 55 us
    pallas_call x1, Pallas kernels: 56 us -> 54.2 us  [local(): pl.pallas_call(kernel, out_shape=(jax.ShapeDtypeStruct((CF, OWN, NX, NY),...]
where the time goes in v6:
time: 57 us; the launch traced here: 56.8 us
  Pallas kernels  55 us (96%)
  between operations  1.8 us (3%)
    pallas_call x1, Pallas kernels, local(): pl.pallas_call(kernel, out_shape=(jax.ShapeDtypeStruct((CF, OWN, NX, NY),...  54.2 us

profile of v6, /device:TPU:1, one launch (start us, length us, event | category | flops | bytes accessed | tf_op | source)
XLA Modules:
  0.0 56.8 jit_solution(780553158409214003)
XLA Ops:
  0.6 54.2 %shard_map.58 = (f32[4,4,64,128]{3,2,1,0:T(8,128)S(1)}, f32[1,4,64,128]{3,2,1,0:T(8,128)S(1)}, f32[1,128]{1,0:T(1,128)S(1)}) custom-call(f32[4,4,64,128]{3,2,1,0:T(8,128)} %state.1, f32[4,4,64,128]{3,2,1,0:T(8,128)} %source.1, f32[4,64,128]{2,1,0:T(8,128)} %absorption.1), custom_call_target="tpu_custom_call" | custom-call | tf_op jit(solution)/shard_map/pallas_call | solution.py:532
  54.8 0.8 %shard_map.59 = (f32[4,4,64,128]{3,2,1,0:T(8,128)}, f32[1,4,64,128]{3,2,1,0:T(8,128)}) custom-call(f32[4,4,64,128]{3,2,1,0:T(8,128)S(1)} %get-tuple-element.8.relaxed, f32[1,4,64,128]{3,2,1,0:T(8,128)S(1)} %get-tuple-element.9.residual), custom_call_target="tpu_custom_call" | custom-call | tf_op jit(solution)/shard_map/pallas_call | solution.py:559

commit v7 on v6

--- a/solution.py
+++ b/solution.py
@@ -330,7 +330,6 @@
     last_step(ALL, ALL, scaled)
     for k in range(OWN):
         d_buf[k] = d_buf[k] + rd[k] * s2_full[k]
-    gather_u.forward()
     phi(scaled)
     for k in range(OWN):
         d_buf[k] = d_buf[k] + rd[k] * s3_own[k]
@@ -350,6 +349,7 @@
             for part in parts:
                 part[0].start()
 
+    gather_u.forward()
     phi(respond, ALL, (8, 9, 10, 11, 6, 7, 12, 13, 0, 1, 2, 3, 4, 5, 14, 15))
     v_copies = [
         remote(v_buf.at[pl.ds(0, 4)], rv_own, v_send.at[0], v_recv.at[0], at(after, d)),
@@ -367,18 +367,6 @@
         copy.start()
         v_copies.append(copy)
 
-    gather_u.middle()
-    gather_u.finish()
-    for z in range(NZ):
-        d_buf[z] = rd[z] * u_full[z]
-
-    def first(z, x):
-        x_buf[4, z] = x
-
-    phi(first)
-    ready_wait(2)
-    ready_signal(3)
-
     for copy in v_copies[:3]:
         copy.wait_recv()
     has_before = jnp.where(c > 0, 1.0, 0.0).astype(jnp.float32)
@@ -397,6 +385,18 @@
         put_natural(stage, point_buf[k], 0, k)
     outs = [pltpu.make_async_copy(stage.at[0], relaxed.at[0], out_sem.at[0])]
     outs[0].start()
+    gather_u.middle()
+    gather_u.finish()
+    for z in range(NZ):
+        d_buf[z] = rd[z] * u_full[z]
+
+    def first(z, x):
+        x_buf[4, z] = x
+
+    phi(first)
+    ready_wait(2)
+    ready_signal(3)
+
     gather_e.forward()
     gather_s1.start()
     gather_e.middle()

time: 57 us -> 55.7 us (0.977)
  Pallas kernels: 55 us -> 53.7 us
    pallas_call x1, Pallas kernels: 54.2 us -> 52.9 us  [local(): pl.pallas_call(kernel, out_shape=(jax.ShapeDtypeStruct((CF, OWN, NX, NY),...]
where the time goes in v7:
time: 55.7 us; the launch traced here: 55.5 us
  Pallas kernels  53.7 us (96%)
  between operations  1.8 us (3%)
    pallas_call x1, Pallas kernels, local(): pl.pallas_call(kernel, out_shape=(jax.ShapeDtypeStruct((CF, OWN, NX, NY),...  52.9 us

profile of v7, /device:TPU:1, one launch (start us, length us, event | category | flops | bytes accessed | tf_op | source)
XLA Modules:
  0.0 55.5 jit_solution(15340489061572610053)
XLA Ops:
  0.6 52.9 %shard_map.58 = (f32[4,4,64,128]{3,2,1,0:T(8,128)S(1)}, f32[1,4,64,128]{3,2,1,0:T(8,128)S(1)}, f32[1,128]{1,0:T(1,128)S(1)}) custom-call(f32[4,4,64,128]{3,2,1,0:T(8,128)} %state.1, f32[4,4,64,128]{3,2,1,0:T(8,128)} %source.1, f32[4,64,128]{2,1,0:T(8,128)} %absorption.1), custom_call_target="tpu_custom_call" | custom-call | tf_op jit(solution)/shard_map/pallas_call | solution.py:532
  53.5 0.8 %shard_map.59 = (f32[4,4,64,128]{3,2,1,0:T(8,128)}, f32[1,4,64,128]{3,2,1,0:T(8,128)}) custom-call(f32[4,4,64,128]{3,2,1,0:T(8,128)S(1)} %get-tuple-element.8.relaxed, f32[1,4,64,128]{3,2,1,0:T(8,128)S(1)} %get-tuple-element.9.residual), custom_call_target="tpu_custom_call" | custom-call | tf_op jit(solution)/shard_map/pallas_call | solution.py:559

commit v8 on v7

--- a/solution.py
+++ b/solution.py
@@ -398,8 +398,8 @@
     ready_signal(3)
 
     gather_e.forward()
+    gather_e.middle()
     gather_s1.start()
-    gather_e.middle()
 
     for z in known:
         d_buf[z] = rd[z] * e_full[z]
@@ -419,9 +419,9 @@
 
     last_step(ALL, ALL, chain(0))
     phi(chain(1))
+    phi(chain(2))
     gather_s1.forward()
     gather_s2.start()
-    phi(chain(2))
     ready_wait(3)
 
     squares = []

time: 55.7 us -> 55.4 us (level)
  no operation moved by 1% of the time
where the time goes in v8:
time: 55.4 us; the launch traced here: 55.3 us
  Pallas kernels  53.5 us (97%)
  between operations  1.8 us (3%)
    pallas_call x1, Pallas kernels, local(): pl.pallas_call(kernel, out_shape=(jax.ShapeDtypeStruct((CF, OWN, NX, NY),...  52.6 us

profile of v8, /device:TPU:1, one launch (start us, length us, event | category | flops | bytes accessed | tf_op | source)
XLA Modules:
  0.0 55.3 jit_solution(17137530205961176752)
XLA Ops:
  0.6 52.6 %shard_map.58 = (f32[4,4,64,128]{3,2,1,0:T(8,128)S(1)}, f32[1,4,64,128]{3,2,1,0:T(8,128)S(1)}, f32[1,128]{1,0:T(1,128)S(1)}) custom-call(f32[4,4,64,128]{3,2,1,0:T(8,128)} %state.1, f32[4,4,64,128]{3,2,1,0:T(8,128)} %source.1, f32[4,64,128]{2,1,0:T(8,128)} %absorption.1), custom_call_target="tpu_custom_call" | custom-call | tf_op jit(solution)/shard_map/pallas_call | solution.py:532
  53.2 0.8 %shard_map.59 = (f32[4,4,64,128]{3,2,1,0:T(8,128)}, f32[1,4,64,128]{3,2,1,0:T(8,128)}) custom-call(f32[4,4,64,128]{3,2,1,0:T(8,128)S(1)} %get-tuple-element.8.relaxed, f32[1,4,64,128]{3,2,1,0:T(8,128)S(1)} %get-tuple-element.9.residual), custom_call_target="tpu_custom_call" | custom-call | tf_op jit(solution)/shard_map/pallas_call | solution.py:559
